TPU v7x, 32 devices: a 4x4x1 block of a 4x4x8 slice. The times are simulated.
32 devices in a mesh: pair: 1 (over z), tp: 4 (over y), side: 8 (over x, core).
Axes of the slice: x: 4, y: 4, z: 1, core: 2. Of those that a mesh axis runs over, the one named last changes fastest.
The devices are a block of a 4x4x8 slice.
Arguments:
- x: bfloat16 [2048, 3072], P(('pair', 'side'))
- req_len: int32 [8], P('pair')
- dest: int32 [8], P('pair')
- w_qkv: bfloat16 [1, 3072, 5120], replicated
- w_out: bfloat16 [1, 3072, 3072], replicated
- w_gate: bfloat16 [1, 3072, 8192], replicated
- w_up: bfloat16 [1, 3072, 8192], replicated
- w_down: bfloat16 [1, 8192, 3072], replicated
- y_tok: bfloat16 [8, 16, 3072], P(('pair', 'side'))
- k_cache: bfloat16 [8, 1, 16, 64, 8, 128], P(('pair', 'side'), None, None, None, 'tp')
- v_cache: bfloat16 [8, 1, 16, 64, 8, 128], P(('pair', 'side'), None, None, None, 'tp')
- c_len: int32 [8, 16], P(('pair', 'side'))
Outputs:
- output 1: bfloat16 [2048, 3072], P(('pair', 'side'))
- output 2: bfloat16 [8, 16, 3072], P(('pair', 'side'))
- output 3: bfloat16 [8, 1, 448, 8, 128], P(('pair', 'side'), None, None, 'tp')
- output 4: bfloat16 [8, 1, 448, 8, 128], P(('pair', 'side'), None, None, 'tp')
- output 5: bfloat16 [8, 1, 16, 64, 8, 128], P(('pair', 'side'), None, None, None, 'tp')
- output 6: bfloat16 [8, 1, 16, 64, 8, 128], P(('pair', 'side'), None, None, None, 'tp')
All inputs are finite; a program needn't handle non-finite values.
Results may differ from a plain program's by a relative error of at most 0.0112437.
Values are sent between devices in bfloat16 or wider.
A program may use at most 768 MiB of HBM per device.

v0:
```python
import jax
import jax.numpy as jnp
from jax import lax
from jax.sharding import PartitionSpec as P

ROPE_BASE = 10000.0
NORM_EPS = 1e-5


def rms_norm(hidden):
    wide_vals = hidden.astype(jnp.float32)
    norm_scale = lax.rsqrt(jnp.mean(wide_vals * wide_vals, axis=-1, keepdims=True) + NORM_EPS)
    return (wide_vals * norm_scale).astype(jnp.bfloat16)


def rotary(vectors, positions):
    half_dim = vectors.shape[-1] // 2
    inv_freq = ROPE_BASE ** (-jnp.arange(half_dim, dtype=jnp.float32) / half_dim)
    angles = positions.astype(jnp.float32)[:, None, None] * inv_freq
    cos_val = jnp.cos(angles)
    sin_val = jnp.sin(angles)
    wide_vals = vectors.astype(jnp.float32)
    lead_half = wide_vals[..., :half_dim]
    tail_half = wide_vals[..., half_dim:]
    return jnp.concatenate([lead_half * cos_val - tail_half * sin_val, tail_half * cos_val + lead_half * sin_val], axis=-1).astype(jnp.bfloat16)


def head_columns(block, groups, tp_size, tp_idx, interleaved):
    row_count, col_count = block.shape
    group_width = col_count // groups
    local_groups = groups // tp_size
    if interleaved:
        head_view = block.reshape(row_count, local_groups, tp_size, group_width)
        return lax.dynamic_index_in_dim(head_view, tp_idx, axis=2, keepdims=False).reshape(row_count, local_groups * group_width)
    return lax.dynamic_slice_in_dim(block, tp_idx * local_groups * group_width, local_groups * group_width, axis=1)


def head_rows(block, groups, tp_size, tp_idx, interleaved):
    row_count, col_count = block.shape
    group_height = row_count // groups
    local_groups = groups // tp_size
    if interleaved:
        head_view = block.reshape(local_groups, tp_size, group_height, col_count)
        return lax.dynamic_index_in_dim(head_view, tp_idx, axis=1, keepdims=False).reshape(local_groups * group_height, col_count)
    return lax.dynamic_slice_in_dim(block, tp_idx * local_groups * group_height, local_groups * group_height, axis=0)


def layer_weights(w_qkv, w_out, w_gate, w_up, w_down, layer, kv_heads, tp_size, tp_idx, interleaved):
    q_cols = w_out.shape[1]
    kv_cols = (w_qkv.shape[2] - q_cols) // 2
    qkv_l = w_qkv[layer]
    wq_l = head_columns(qkv_l[:, :q_cols], kv_heads, tp_size, tp_idx, interleaved)
    wk_l = head_columns(qkv_l[:, q_cols:q_cols + kv_cols], kv_heads, tp_size, tp_idx, interleaved)
    wv_l = head_columns(qkv_l[:, q_cols + kv_cols:], kv_heads, tp_size, tp_idx, interleaved)
    wo_l = head_rows(w_out[layer], kv_heads, tp_size, tp_idx, interleaved)
    ff_local = w_gate.shape[2] // tp_size
    wg_l = lax.dynamic_slice_in_dim(w_gate[layer], tp_idx * ff_local, ff_local, axis=1)
    wu_l = lax.dynamic_slice_in_dim(w_up[layer], tp_idx * ff_local, ff_local, axis=1)
    wd_l = lax.dynamic_slice_in_dim(w_down[layer], tp_idx * ff_local, ff_local, axis=0)
    return wq_l, wk_l, wv_l, wo_l, wg_l, wu_l, wd_l


def project(hidden, wq_l, wk_l, wv_l, positions, kv_local, group_rep):
    row_count = hidden.shape[0]
    head_dim = wk_l.shape[1] // kv_local
    normed = rms_norm(hidden)
    query = jnp.dot(normed, wq_l, preferred_element_type=jnp.float32).astype(jnp.bfloat16)
    key_new = jnp.dot(normed, wk_l, preferred_element_type=jnp.float32).astype(jnp.bfloat16)
    value_new = jnp.dot(normed, wv_l, preferred_element_type=jnp.float32).astype(jnp.bfloat16)
    query = rotary(query.reshape(row_count, kv_local * group_rep, head_dim), positions)
    key_new = rotary(key_new.reshape(row_count, kv_local, head_dim), positions)
    return query.reshape(row_count, kv_local, group_rep, head_dim), key_new, value_new.reshape(row_count, kv_local, head_dim)


def finish_layer(hidden, context, wo_l, wg_l, wu_l, wd_l):
    attn_out = lax.psum(jnp.dot(context, wo_l, preferred_element_type=jnp.float32), 'tp').astype(jnp.bfloat16)
    hidden = (hidden.astype(jnp.float32) + attn_out.astype(jnp.float32)).astype(jnp.bfloat16)
    normed = rms_norm(hidden)
    gate = jnp.dot(normed, wg_l, preferred_element_type=jnp.float32).astype(jnp.bfloat16)
    upper = jnp.dot(normed, wu_l, preferred_element_type=jnp.float32).astype(jnp.bfloat16)
    activated = (jax.nn.silu(gate.astype(jnp.float32)) * upper.astype(jnp.float32)).astype(jnp.bfloat16)
    down = lax.psum(jnp.dot(activated, wd_l, preferred_element_type=jnp.float32), 'tp').astype(jnp.bfloat16)
    return (hidden.astype(jnp.float32) + down.astype(jnp.float32)).astype(jnp.bfloat16)


def prompt_attention(query, key_new, value_new, allowed):
    score_scale = query.shape[-1] ** -0.5
    scores = jnp.einsum('sjrd,tjd->jrst', query, key_new, preferred_element_type=jnp.float32) * score_scale
    scores = jnp.where(allowed, scores, -1e30)
    attn_prob = jax.nn.softmax(scores, axis=-1).astype(jnp.bfloat16)
    context = jnp.einsum('jrst,tjd->sjrd', attn_prob, value_new, preferred_element_type=jnp.float32).astype(jnp.bfloat16)
    return context.reshape(query.shape[0], -1)


def decode_attention(query, k_layer, v_layer, lengths):
    score_scale = query.shape[-1] ** -0.5
    cache_pos = jnp.arange(k_layer.shape[1])
    visible = cache_pos[None, :] <= lengths[:, None]
    scores = jnp.einsum('bjrd,btjd->bjrt', query, k_layer, preferred_element_type=jnp.float32) * score_scale
    scores = jnp.where(visible[:, None, None, :], scores, -1e30)
    attn_prob = jax.nn.softmax(scores, axis=-1).astype(jnp.bfloat16)
    context = jnp.einsum('bjrt,btjd->bjrd', attn_prob, v_layer, preferred_element_type=jnp.float32).astype(jnp.bfloat16)
    return context.reshape(query.shape[0], -1)


def write_slot(cache, row_new, lengths):
    return jax.vmap(lambda one_cache, one_row, one_len: lax.dynamic_update_slice_in_dim(one_cache, one_row[None], one_len, axis=0))(cache, row_new, lengths)


def segments(req_len, seq_len):
    row_ids = jnp.arange(seq_len)
    past_end = row_ids[:, None] >= jnp.cumsum(req_len)[None, :]
    seg_id = jnp.sum(past_end.astype(jnp.int32), axis=1)
    positions = row_ids - jnp.sum(jnp.where(past_end, req_len[None, :], 0), axis=1)
    allowed = (seg_id[:, None] == seg_id[None, :]) & (row_ids[None, :] <= row_ids[:, None])
    return positions, allowed


def pick_interleaved(full, tp_size, tp_idx):
    shape_in = full.shape
    head_view = full.reshape(shape_in[:2] + (shape_in[2] // tp_size, tp_size) + shape_in[3:])
    return lax.dynamic_index_in_dim(head_view, tp_idx, axis=3, keepdims=False)


def request_pieces(full, req_len, dest, max_req):
    side_size = req_len.shape[0]
    starts = jnp.cumsum(req_len) - req_len
    match = dest[None, :] == jnp.arange(side_size)[:, None]
    start_of = jnp.sum(jnp.where(match, starts[None, :], 0), axis=1)
    length_of = jnp.sum(jnp.where(match, req_len[None, :], 0), axis=1)
    padded = jnp.concatenate([full, jnp.zeros((full.shape[0], max_req) + full.shape[2:], full.dtype)], axis=1)

    def one_group(start_row, length):
        piece = lax.dynamic_slice_in_dim(padded, start_row, max_req, axis=1)
        keep = (jnp.arange(max_req) < length)[None, :, None, None]
        return jnp.where(keep, piece, jnp.zeros_like(piece))

    return jax.vmap(one_group)(start_of, length_of)


def solution(mesh):
    tp_size = mesh.shape['tp']
    side_size = mesh.shape['side']
    rows_spec = P(('pair', 'side'), None)
    batch_spec = P(('pair', 'side'), None, None)
    cache_spec = P(('pair', 'side'), None, None, None, 'tp', None)
    prompt_spec = P(('pair', 'side'), None, None, 'tp', None)

    def local_step(x_loc, req_len, dest, w_qkv, w_out, w_gate, w_up, w_down, y_loc, kc_loc, vc_loc, clen_loc):
        side_idx = lax.axis_index('side')
        tp_idx = lax.axis_index('tp')
        layers = w_qkv.shape[0]
        head_dim = kc_loc.shape[-1]
        kv_local = kc_loc.shape[-2]
        kv_heads = kv_local * tp_size
        group_rep = w_out.shape[1] // head_dim // kv_heads
        prompt_rows, model_dim = x_loc.shape
        seq_len = prompt_rows * side_size
        max_req = 2 * prompt_rows - prompt_rows // 4

        x_full = lax.all_gather(x_loc, 'side', axis=0, tiled=True)
        positions, allowed = segments(req_len, seq_len)

        def run_prefill(x_rows):
            hidden = x_rows
            keys_all = []
            values_all = []
            for layer in range(layers):
                wq_l, wk_l, wv_l, wo_l, wg_l, wu_l, wd_l = layer_weights(w_qkv, w_out, w_gate, w_up, w_down, layer, kv_heads, tp_size, tp_idx, False)
                query, key_new, value_new = project(hidden, wq_l, wk_l, wv_l, positions, kv_local, group_rep)
                keys_all.append(key_new)
                values_all.append(value_new)
                context = prompt_attention(query, key_new, value_new, allowed)
                hidden = finish_layer(hidden, context, wo_l, wg_l, wu_l, wd_l)
            return hidden, jnp.stack(keys_all), jnp.stack(values_all)

        def skip_prefill(x_rows):
            kv_shape = (layers, seq_len, kv_local, head_dim)
            return jnp.zeros_like(x_rows), jnp.zeros(kv_shape, jnp.bfloat16), jnp.zeros(kv_shape, jnp.bfloat16)

        hidden, keys_loc, values_loc = lax.cond(side_idx == 0, run_prefill, skip_prefill, x_full)
        keys_full = lax.all_gather(keys_loc, 'tp', axis=2, tiled=True)
        values_full = lax.all_gather(values_loc, 'tp', axis=2, tiled=True)
        k_send = request_pieces(pick_interleaved(keys_full, tp_size, tp_idx), req_len, dest, max_req)
        v_send = request_pieces(pick_interleaved(values_full, tp_size, tp_idx), req_len, dest, max_req)
        k_recv = lax.all_to_all(k_send, 'side', 0, 0, tiled=True)[0]
        v_recv = lax.all_to_all(v_send, 'side', 0, 0, tiled=True)[0]
        hidden_rows = lax.all_to_all(hidden.reshape(side_size, prompt_rows, model_dim), 'side', 0, 0, tiled=True)[0]

        lengths = clen_loc[0]
        hidden_dec = y_loc[0]
        k_out = []
        v_out = []
        for layer in range(layers):
            wq_l, wk_l, wv_l, wo_l, wg_l, wu_l, wd_l = layer_weights(w_qkv, w_out, w_gate, w_up, w_down, layer, kv_heads, tp_size, tp_idx, True)
            query, key_new, value_new = project(hidden_dec, wq_l, wk_l, wv_l, lengths, kv_local, group_rep)
            k_layer = write_slot(kc_loc[0, layer], key_new, lengths)
            v_layer = write_slot(vc_loc[0, layer], value_new, lengths)
            context = decode_attention(query, k_layer, v_layer, lengths)
            hidden_dec = finish_layer(hidden_dec, context, wo_l, wg_l, wu_l, wd_l)
            k_out.append(k_layer)
            v_out.append(v_layer)
        return hidden_rows, hidden_dec[None], k_recv[None], v_recv[None], jnp.stack(k_out)[None], jnp.stack(v_out)[None]

    return jax.shard_map(local_step, mesh=mesh,
                         in_specs=(rows_spec, P('pair'), P('pair'), P(), P(), P(), P(), P(), batch_spec, cache_spec, cache_spec, rows_spec),
                         out_specs=(rows_spec, batch_spec, prompt_spec, prompt_spec, cache_spec, cache_spec),
                         check_vma=False)
```

profile of v0, /device:TPU:97, one launch (start us, length us, event | category | flops | bytes accessed | tf_op | source)
XLA Modules:
  0.0 1362.4 jit_solution(6572397708470487288)
XLA Ops:
  9.0 69.8 %all-gather.4.cloned.1.call-done = bf16[2048,3072]{1,0:T(8,128)(2,1)} async-done(((bf16[256,3072]{1,0:T(8,128)(2,1)}), bf16[2048,3072]{1,0:T(8,128)(2,1)}) %all-gather.4.cloned.1.call-update) | async-done | bytes 12582928 | tf_op jit(solution)/shard_map/all_gather | solution.py:161
  78.7 6.8 le.32
  85.5 7.8 le.33
  93.4 15.3 %conditional.1 = (bf16[2048,3072]{1,0:T(8,128)(2,1)}, bf16[1,2048,2,128]{3,1,2,0:T(8,128)(2,1)}, bf16[1,2048,2,128]{1,3,2,0:T(8,128)(2,1)S(1)}) conditional(s32[]{:T(128)} %convert_element_type.202, () %tuple.16, (bf16[2048,3072]{1,0:T(8,128)(2,1)}, bf16[1,3072,5120]{2,1,0:T(8,128)(2,1)}, s32[]{:T(128)}, s32[2048,8]{0,1:T(8,128)S(1)}, ...), branch_computations={%region_3.4_spmd, %region_4.11_spmd} | conditional | flops 122907459584 | bytes 610599808 | solution.py:181
  93.4 6.1 broadcast.267
  110.3 40.7 %copy.129 = bf16[1,3072,5120]{1,2,0:T(8,128)(2,1)} copy(bf16[1,3072,5120]{2,1,0:T(8,128)(2,1)} %param.17) | data formatting | bytes 62914560 | tf_op args[3]
  151.3 5.6 fusion.152
  158.8 791.7 %all-gather.6.cloned.1.call-done = bf16[1,2048,8,128]{3,1,0,2:T(8,128)(2,1)} async-done(((bf16[1,2048,2,128]{3,1,0,2:T(8,128)(2,1)}), bf16[1,2048,8,128]{3,1,0,2:T(8,128)(2,1)}) %all-gather.6.cloned.1.call-update) | async-done | bytes 4194320 | tf_op jit(solution)/shard_map/all_gather | solution.py:182
  950.5 47.5 %all-gather.8.cloned.1.call-done = bf16[1,2048,8,128]{3,1,0,2:T(8,128)(2,1)} async-done(((bf16[1,2048,2,128]{3,1,0,2:T(8,128)(2,1)}), bf16[1,2048,8,128]{3,1,0,2:T(8,128)(2,1)}) %all-gather.8.cloned.1.call-update) | async-done | bytes 4194320 | tf_op jit(solution)/shard_map/all_gather | solution.py:183
  999.7 8.7 copy.157
  1008.4 8.7 copy.158
  1024.5 5.4 gather_fusion.1
  1034.1 9.6 fusion.98
  1043.8 5.3 all-to-all-start.1
  1051.5 20.8 %all-to-all-done.1 = bf16[8,1,448,2,128]{4,3,2,1,0:T(2,128)(2,1)S(1)} async-done(((bf16[8,1,448,2,128]{4,3,2,1,0:T(2,128)(2,1)}), bf16[8,1,448,2,128]{4,3,2,1,0:T(2,128)(2,1)S(1)}, u32[]{:S(2)}, u32[]{:S(2)}) %all-to-all-start.1) | async-done | bytes 1835040 | tf_op jit(solution)/shard_map/all_to_all | solution.py:186
  1072.3 5.8 all-to-all-start.2
  1078.1 96.8 %while.2 = (s32[]{:T(128)}, bf16[16,64,2,128]{3,2,1,0:T(2,128)(2,1)S(1)}, s32[16,4]{0,1:T(4,128)S(1)}, bf16[16,1,2,128]{3,2,1,0:T(2,128)(2,1)S(1)}, s32[]{:T(128)}, /*index=5*/s32[4]{0:T(128)S(1)}) while((s32[]{:T(128)}, bf16[16,64,2,128]{3,2,1,0:T(2,128)(2,1)S(1)}, s32[16,4]{0,1:T(4,128)S(1)}, bf16[16,1,2,128]{3,2,1,0:T(2,128)(2,1)S(1)}, s32[]{:T(128)}, ...), condition=%wide.while_cond, body=%wide.while_body.sunk | while | flops 285 | bytes 1727 | solution.py:107
  1174.9 17.0 %slice.125 = bf16[3072,3072]{0,1:T(8,128)(2,1)} slice(bf16[3072,5120]{0,1:T(8,128)(2,1)} %bitcast.220), slice={[0:3072], [0:3072]} | slice | bytes 37748736 | tf_op jit(solution)/shard_map/slice | solution.py:52
  1196.6 5.5 all-to-all-start
  1204.0 94.7 %while.3 = (s32[]{:T(128)}, bf16[16,64,2,128]{3,2,1,0:T(2,128)(2,1)S(1)}, s32[16,4]{0,1:T(4,128)S(1)}, bf16[16,1,2,128]{3,2,1,0:T(2,128)(2,1)S(1)}, s32[]{:T(128)}, /*index=5*/s32[4]{0:T(128)S(1)}) while((s32[]{:T(128)}, bf16[16,64,2,128]{3,2,1,0:T(2,128)(2,1)S(1)}, s32[16,4]{0,1:T(4,128)S(1)}, bf16[16,1,2,128]{3,2,1,0:T(2,128)(2,1)S(1)}, ...), condition=%wide.while_cond.1, body=%wide.while_body.1.sunk | while | flops 285 | bytes 1727 | solution.py:107
  1302.6 15.3 %all-reduce.9 = bf16[16,3072]{1,0:T(8,128)(2,1)S(1)} all-reduce(f32[16,3072]{1,0:T(8,128)S(1)} %fusion.154), channel_id=1, replica_groups=mesh['pair'=1,'tp'=4,'side'=8] {'tp'}, use_global_device_ids=true, to_apply=%region_16.17 | all-reduce | flops 49152 | bytes 294912 | tf_op jit(solution)/shard_map/psum | solution.py:76
  1318.1 6.4 fusion.82
  1324.4 11.6 fusion.70
  1336.0 13.5 all-reduce.10
  (215 shorter events, 229.8 us)
Async XLA Ops:
  7.2 71.6 %all-gather.4.cloned.1.call-start = ((), (), s32[]{:S(2)}) async-start(), calls=%async_computation.3 | async-start | bytes 14155776 | tf_op jit(solution)/shard_map/all_gather | solution.py:161
  8.0 942.6 %all-gather.6.cloned.1.call-start = ((), (), s32[]{:S(2)}) async-start(), calls=%async_computation.4 | async-start | bytes 5242880 | tf_op jit(solution)/shard_map/all_gather | solution.py:182
  8.9 76.6 %copy-start.20 = (s32[8,1]{0,1:T(1,128)}, s32[8,1]{0,1:T(1,128)S(1)}, u32[]{:S(2)}) copy-start(s32[8,1]{0,1:T(1,128)S(1)} %reduce-window.8) | copy-start | bytes 100
  85.5 7.8 copy-start.18
  108.7 889.3 %all-gather.8.cloned.1.call-start = ((), (), s32[]{:S(2)}) async-start(), calls=%async_computation.5 | async-start | bytes 5242880 | tf_op jit(solution)/shard_map/all_gather | solution.py:183
  110.2 40.7 %copy-start.19 = (s32[8]{0:T(128)S(1)}, s32[8]{0:T(128)}, u32[]{:S(2)}) copy-start(s32[8]{0:T(128)} %param.15) | copy-start | bytes 100
  110.2 40.7 %copy-start.21 = (s32[8,1]{0,1:T(1,128)S(1)}, s32[8,1]{0,1:T(1,128)}, u32[]{:S(2)}) copy-start(s32[8,1]{0,1:T(1,128)} %copy-done.20) | copy-start | bytes 100
  110.2 40.7 %copy-start.22 = (s32[8]{0:T(128)S(1)}, s32[8]{0:T(128)}, u32[]{:S(2)}) copy-start(s32[8]{0:T(128)} %param.16) | copy-start | bytes 100
  110.2 40.8 %copy-start.12 = (bf16[1,16,3072]{2,1,0:T(8,128)(2,1)S(1)}, bf16[1,16,3072]{2,1,0:T(8,128)(2,1)}, u32[]{:S(2)}) copy-start(bf16[1,16,3072]{2,1,0:T(8,128)(2,1)} %param.22) | copy-start | bytes 294916
  1034.1 17.0 %copy-start.23 = (s32[1,16]{1,0:T(1,128)S(1)}, s32[1,16]{1,0:T(1,128)}, u32[]{:S(2)}) copy-start(s32[1,16]{1,0:T(1,128)} %param.25) | copy-start | bytes 196
  1034.1 17.0 %copy-start.24 = (s32[3]{0:T(128)S(1)}, s32[3]{0:T(128)}, u32[]{:S(2)}) copy-start(s32[3]{0:T(128)} %constant.118.clone.1) | copy-start | bytes 40
  1043.7 34.3 %copy-start.16 = (bf16[1,1,16,64,2,128]{5,4,3,2,1,0:T(2,128)(2,1)S(1)}, bf16[1,1,16,64,2,128]{5,4,3,2,1,0:T(2,128)(2,1)}, u32[]{:S(2)}) copy-start(bf16[1,1,16,64,2,128]{5,4,3,2,1,0:T(2,128)(2,1)} %param.23) | copy-start | bytes 1572868
  1043.7 34.3 %copy-start.17 = (s32[4]{0:T(128)S(1)}, s32[4]{0:T(128)}, u32[]{:S(2)}) copy-start(s32[4]{0:T(128)} %constant.403) | copy-start | bytes 52
  1043.8 28.5 %all-to-all-start.1 = ((bf16[8,1,448,2,128]{4,3,2,1,0:T(2,128)(2,1)}), bf16[8,1,448,2,128]{4,3,2,1,0:T(2,128)(2,1)S(1)}, u32[]{:S(2)}, u32[]{:S(2)}) async-start(bf16[8,1,448,2,128]{4,3,2,1,0:T(2,128)(2,1)} %get-tuple-element.181), calls=%async_computation.1 | async-start | bytes 3670016 | tf_op jit(solution)/shard_map/all_to_all | solution.py:186
  1072.3 124.3 %all-to-all-start.2 = ((bf16[8,1,448,2,128]{4,3,2,1,0:T(2,128)(2,1)}), bf16[8,1,448,2,128]{4,3,2,1,0:T(2,128)(2,1)}, u32[]{:S(2)}, u32[]{:S(2)}) async-start(bf16[8,1,448,2,128]{4,3,2,1,0:T(2,128)(2,1)} %get-tuple-element.180), calls=%async_computation.2 | async-start | bytes 3670016 | tf_op jit(solution)/shard_map/all_to_all | solution.py:187
  1174.9 17.0 %copy-start.15 = (bf16[16,64,2,128]{3,2,1,0:T(2,128)(2,1)}, bf16[16,64,2,128]{3,2,1,0:T(2,128)(2,1)S(1)}, u32[]{:S(2)}) copy-start(bf16[16,64,2,128]{3,2,1,0:T(2,128)(2,1)S(1)} %get-tuple-element.61) | copy-start | bytes 1572868
  1174.9 17.0 %copy-start.1 = (bf16[3072,2,1,128]{0,3,2,1:T(8,128)(2,1)S(1)}, bf16[3072,2,1,128]{0,3,2,1:T(8,128)(2,1)}, u32[]{:S(2)}) copy-start(bf16[3072,2,1,128]{0,3,2,1:T(8,128)(2,1)} %get-tuple-element.188) | copy-start | bytes 4718596
  1196.6 7.3 copy-start.14
  1196.6 156.1 %all-to-all-start = ((bf16[8,256,3072]{2,1,0:T(8,128)(2,1)}), bf16[8,256,3072]{2,1,0:T(8,128)(2,1)}, u32[]{:S(2)}, u32[]{:S(2)}) async-start(bf16[8,256,3072]{2,1,0:T(8,128)(2,1)} %bitcast.221), calls=%async_computation | async-start | bytes 25165824 | tf_op jit(solution)/shard_map/all_to_all | solution.py:188
  1298.6 4.0 copy-start.13
Sparse Core Ops, SparseCore 0:
  9.6 69.0 all-gather.3
  108.9 841.6 all-gather.5
  952.1 45.9 all-gather.7
where the time goes:
time: 1370 us; the launch traced here: 1360 us
  waiting for transfers between devices  931 us (68%)
  other arithmetic  182 us (13%)
  local copies, waits for them, and re-layouts  156 us (11%)
  blocking collectives  28.8 us (2%)
  matrix products  24.4 us (2%)
  starting transfers between devices  16.8 us (1%)
  between operations  14.6 us (1%)
    all_gather x1, waiting for transfers between devices, local_step(): keys_full = lax.all_gather(keys_loc, 'tp', axis=2, tiled=True)  792 us
    scatter x64, other arithmetic  170 us
    all_gather x1, waiting for transfers between devices, local_step(): x_full = lax.all_gather(x_loc, 'side', axis=0, tiled=True)  69.8 us
    unnamed x32, local copies, waits for them, and re-layouts  58.1 us
    all_gather x1, waiting for transfers between devices, local_step(): values_full = lax.all_gather(values_loc, 'tp', axis=2, tiled=True)  47.5 us
  transfers between devices with their start and end apart: 6, of which 4 were waited for; matrix products, arithmetic and copies ran while one was open for 21% of the time, Pallas kernels for 0%

commit v1 on v0

v1 whole, which is shorter than its diff:
```python
import jax
import jax.numpy as jnp
from jax import lax
from jax.experimental import pallas as pl
from jax.experimental.pallas import tpu as pltpu
from jax.sharding import PartitionSpec as P

ROPE_BASE = 10000.0
NORM_EPS = 1e-5
BF = jnp.bfloat16
F32 = jnp.float32
CW = 256
GU_SLOTS = 8
MESH = pl.DeviceIdType.MESH


def mult(v, m):
    return pl.multiple_of(v, m)


def make_kernel(tp_size, side_size, R, D, B, T, Q, KV, HD, F, max_req):
    heads_local = Q // HD // tp_size
    rep = heads_local // 2
    hw = rep * HD
    qw = 2 * hw
    RT = R // tp_size
    DH = D // 2
    FH = F // 2
    M1 = R + B
    M2 = 2 * RT + 2 * B
    n_kv, n_q = 2 * 2 * HD // CW, qw // CW
    n_o, n_g, n_d = DH // CW, FH // CW, DH // CW
    wo_base = (n_kv + n_q) * D
    gu_base = wo_base + n_o * Q
    slab_rows = gu_base + GU_SLOTS * 2 * D
    CK = B * T * 2
    PR = max_req * 2
    scale = HD ** -0.5
    nblk = side_size

    def kernel(x_h, y_h, wqkv_h, wo_h, wg_h, wu_h, wd_h, kc_h, vc_h, rl, dst, cl, fq,
               hid_o, dec_o, kp_o, vp_o, kn_o, vn_o,
               slab, xs, ys, xn, raw, qs, kva, knv, kcs, vcs, cos_s, sin_s,
               dcs, cst, ctxr, xres, hf, hn, act, outst, hid, decb, kps, vps,
               in_sem, w_sem, g_sem, d_sem, xr_s, xr_r, kx_s, kx_r, cx_s, cx_r, cf_s, cf_r,
               dx_s, dx_r, df_s, df_r, h_s, h_r, a_s, a_r, f_s, f_r, r_s, r_r, o_sem):
        side = lax.axis_index('side')
        tp = lax.axis_index('tp')
        core = lax.rem(side, 2)
        oc = 1 - core
        partner = side + 1 - 2 * core
        left = lax.rem(side + side_size - 2, side_size)
        right = lax.rem(side + 2, side_size)
        far = lax.rem(side + 4, side_size)
        p_left = lax.rem(partner + side_size - 2, side_size)
        p_right = lax.rem(partner + 2, side_size)
        p_far = lax.rem(partner + 4, side_size)

        def at(d):
            return lax.rem(tp + d, tp_size)

        def dev(s, t):
            return {'side': s, 'tp': t}

        q_cols0, k_cols0, v_cols0 = 0, Q, Q + KV
        hcol = [tp * hw, (tp + tp_size) * hw]
        kcol = [k_cols0 + tp * HD, k_cols0 + (tp + tp_size) * HD]
        vcol = [v_cols0 + tp * HD, v_cols0 + (tp + tp_size) * HD]

        def pieces(u):
            if u == 0:
                return [(kcol[0], 0, HD), (kcol[1], HD, HD)]
            if u == 1:
                return [(vcol[0], 0, HD), (vcol[1], HD, HD)]
            lo, hi = (u - 2) * CW, (u - 1) * CW
            out = []
            for j in range(2):
                a, b = max(lo, j * hw), min(hi, (j + 1) * hw)
                if a < b:
                    out.append((hcol[j] + (a - j * hw), a - lo, b - a))
            return out

        def start_qkv(u):
            for src, d0, w in pieces(u):
                pltpu.make_async_copy(wqkv_h.at[:, pl.ds(mult(src, 128), w)],
                                      slab.at[pl.ds(u * D, D), pl.ds(d0, w)], w_sem.at[u]).start()

        def slab_wait(base, rows, sem):
            pltpu.make_async_copy(slab.at[pl.ds(base, rows), :], slab.at[pl.ds(base, rows), :], sem).wait()

        def start_wo(u):
            col = mult(core * DH + u * CW, 128)
            for t in range(tp_size):
                for j in range(2):
                    pltpu.make_async_copy(wo_h.at[pl.ds((t + j * tp_size) * hw, hw), pl.ds(col, CW)],
                                          slab.at[pl.ds(wo_base + u * Q + t * qw + j * hw, hw), :],
                                          w_sem.at[n_kv + n_q + u]).start()

        def start_gu(j, slot):
            col = mult(core * FH + j * CW, 128)
            base = mult(gu_base + slot * (2 * D), 256)
            pltpu.make_async_copy(wg_h.at[:, pl.ds(col, CW)], slab.at[pl.ds(base, D), :], g_sem.at[slot]).start()
            pltpu.make_async_copy(wu_h.at[:, pl.ds(col, CW)], slab.at[pl.ds(mult(base + D, 256), D), :], g_sem.at[slot]).start()

        def d_copy(n):
            return pltpu.make_async_copy(wd_h.at[:, pl.ds(mult(core * DH + n * CW, 128), CW)],
                                         slab.at[pl.ds(mult(n * F, 256), F), :], d_sem.at[n])

        x_in = pltpu.make_async_copy(x_h, xs, in_sem.at[0])
        y_in = pltpu.make_async_copy(y_h, ys, in_sem.at[1])
        x_in.start()
        y_in.start()
        for u in range(n_kv + n_q):
            start_qkv(u)

        peers = [(partner, tp), (left, tp), (right, tp), (side, at(1)), (side, at(tp_size - 1)), (side, at(2)),
                 (partner, at(1)), (partner, at(tp_size - 1))]
        barrier = pltpu.get_barrier_semaphore()
        for s, t in peers:
            pl.semaphore_signal(barrier, inc=1, device_id=dev(s, t), device_id_type=MESH)

        kc_in = pltpu.make_async_copy(kc_h, kcs, in_sem.at[2])
        vc_in = pltpu.make_async_copy(vc_h, vcs, in_sem.at[3])
        kc_in.start()
        vc_in.start()
        row_t = mult(tp * RT, RT)
        my_cols = mult(core * DH, 128)
        xres_l = [pltpu.make_async_copy(x_h.at[pl.ds(row_t, RT), pl.ds(my_cols, DH)],
                                        xres.at[pl.ds(mult(core * RT, RT), RT), :], in_sem.at[4]),
                  pltpu.make_async_copy(y_h.at[:, pl.ds(my_cols, DH)],
                                        xres.at[pl.ds(mult(2 * RT + core * B, B), B), :], in_sem.at[5])]
        for cp in xres_l:
            cp.start()

        def seg_of(rows):
            seg = jnp.zeros_like(rows)
            total = jnp.int32(0)
            for r in range(nblk):
                total = total + rl[r]
                seg = jnp.where(rows >= total, total, seg)
            return seg

        idx = lax.broadcasted_iota(jnp.int32, (M1, 1), 0)
        rows = idx + side * R
        pos = rows - seg_of(rows)
        for b in range(B):
            pos = jnp.where(idx == R + b, cl[b], pos)
        ang = pos.astype(F32) * fq[0:1, :]
        cos_s[...] = jnp.cos(ang)
        sin_s[...] = jnp.sin(ang) * fq[1:2, :]

        def norm(v):
            w = v.astype(F32)
            sc = lax.rsqrt(jnp.sum(w * w, axis=-1, keepdims=True) / D + NORM_EPS)
            return (w * sc).astype(BF)

        x_in.wait()

        def norm_x(i, c):
            r = pl.ds(mult(i * 32, 32), 32)
            xn[r, :] = norm(xs[r, :])
            return c

        lax.fori_loop(0, R // 32, norm_x, 0)
        y_in.wait()
        xn[pl.ds(R, B), :] = norm(ys[...])

        pl.semaphore_wait(barrier, len(peers))

        def remote(src, dst_ref, ss, rs, s, t):
            return pltpu.make_async_remote_copy(src_ref=src, dst_ref=dst_ref, send_sem=ss, recv_sem=rs,
                                                device_id=dev(s, t), device_id_type=MESH)

        his_cols = mult(oc * DH, 128)
        xres_r = [remote(x_h.at[pl.ds(row_t, RT), pl.ds(his_cols, DH)], xres.at[pl.ds(mult(core * RT, RT), RT), :],
                         xr_s.at[0], xr_r.at[0], partner, tp),
                  remote(y_h.at[:, pl.ds(his_cols, DH)], xres.at[pl.ds(mult(2 * RT + core * B, B), B), :],
                         xr_s.at[1], xr_r.at[1], partner, tp)]
        for cp in xres_r:
            cp.start()

        def project(u):
            w = slab[pl.ds(mult(u * D, 256), D), :]
            raw[u] = jnp.dot(xn[...], w, preferred_element_type=F32).astype(BF)

        def rope(v):
            w = v.astype(F32)
            return (w * cos_s[...] + pltpu.roll(w, HD // 2, 1) * sin_s[...]).astype(BF)

        def project_loop(i, c):
            slab_wait(mult(i * D, 256), D, w_sem.at[i])
            project(i)
            return c

        for u in range(n_o):
            start_wo(u)
        lax.fori_loop(0, n_kv, project_loop, 0)
        for j in range(2):
            k_j = rope(raw[0, :, pl.ds(j * HD, HD)])
            kva[side, j] = k_j[:R]
            knv[pl.ds(j * B, B), pl.ds(0, HD)] = k_j[R:]
            v_j = raw[1, :, pl.ds(j * HD, HD)]
            kva[side, 2 + j] = v_j[:R]
            knv[pl.ds(j * B, B), pl.ds(HD, HD)] = v_j[R:]
        knv[:, pl.ds(2 * HD, HD)] = jnp.ones((2 * B, HD), BF)

        lo, hi = pl.ds(0, 2), pl.ds(2, 2)
        kx = [remote(kva.at[side], kva.at[side], kx_s.at[0], kx_r.at[0], partner, tp),
              remote(kva.at[side], kva.at[side], kx_s.at[1], kx_r.at[1], right, tp),
              remote(kva.at[side], kva.at[side], kx_s.at[2], kx_r.at[2], left, tp),
              remote(kva.at[left, lo], kva.at[left, lo], kx_s.at[3], kx_r.at[3], right, tp),
              remote(kva.at[right, hi], kva.at[right, hi], kx_s.at[4], kx_r.at[4], left, tp),
              remote(kva.at[left], kva.at[left], kx_s.at[5], kx_r.at[5], partner, tp),
              remote(kva.at[right], kva.at[right], kx_s.at[6], kx_r.at[6], partner, tp),
              remote(kva.at[far, lo], kva.at[far, lo], kx_s.at[7], kx_r.at[7], partner, tp),
              remote(kva.at[far, hi], kva.at[far, hi], kx_s.at[8], kx_r.at[8], partner, tp)]
        for i in (1, 0, 2):
            kx[i].start()

        def got(i):
            blk = (partner, left, right, far, far, p_left, p_right, p_far, p_far)[i]
            ref = kva.at[blk, lo] if i in (3, 7) else kva.at[blk, hi] if i in (4, 8) else kva.at[blk]
            pltpu.make_async_copy(ref, ref, kx_r.at[i]).wait()

        lax.fori_loop(n_kv, n_kv + n_q, project_loop, 0)
        for slot in range(GU_SLOTS):
            start_gu(slot, slot)
        d_copy(0).start()
        for h in range(heads_local):
            u, off = divmod(h * HD, CW)
            qs[h] = rope(raw[2 + u, :, pl.ds(off, HD)])

        kc_in.wait()
        vc_in.wait()
        lane2 = lax.broadcasted_iota(jnp.int32, (1, 2 * B), 1)
        len2 = jnp.zeros((1, 2 * B), jnp.int32)
        for b in range(B):
            len2 = jnp.where(lax.rem(lane2, B) == b, cl[b], len2)
        code2 = (lax.rem(lane2, B) * T + len2) * 2 + lane2 // B
        CH = 256

        def insert(i, c):
            r0 = mult(i * CH, CH)
            rr = lax.broadcasted_iota(jnp.int32, (CH, 1), 0) + r0
            pick = jnp.where(rr == code2, 1.0, 0.0).astype(BF)
            new = jnp.dot(pick, knv[...], preferred_element_type=F32)
            hit = new[:, 2 * HD:] > 0.5
            sl = pl.ds(r0, CH)
            kcs[sl, :] = jnp.where(hit, new[:, :HD], kcs[sl, :].astype(F32)).astype(BF)
            vcs[sl, :] = jnp.where(hit, new[:, HD:2 * HD], vcs[sl, :].astype(F32)).astype(BF)
            return c

        lax.fori_loop(0, CK // CH, insert, 0)
        kn_out = pltpu.make_async_copy(kcs, kn_o, o_sem.at[0])
        vn_out = pltpu.make_async_copy(vcs, vn_o, o_sem.at[1])
        kn_out.start()
        vn_out.start()

        HB = heads_local * B
        q_dec = qs[:, pl.ds(R, B), :].reshape(HB, HD)
        s_dec = lax.dot_general(q_dec, kcs[...], (((1,), (1,)), ((), ())), preferred_element_type=F32) * scale
        qi = lax.broadcasted_iota(jnp.int32, (HB, 1), 0)
        ki = lax.broadcasted_iota(jnp.int32, (1, CK), 1)
        q_len = jnp.zeros((HB, 1), jnp.int32)
        for b in range(B):
            q_len = jnp.where(lax.rem(qi, B) == b, cl[b], q_len)
        q_code = lax.rem(qi, B) * 2 + qi // (rep * B)
        k_code = (ki // (2 * T)) * 2 + lax.rem(ki, 2)
        k_pos = lax.rem(ki // 2, T)
        s_dec = jnp.where((q_code == k_code) & (k_pos <= q_len), s_dec, -1e30)
        e_dec = jnp.exp(s_dec - jnp.max(s_dec, axis=-1, keepdims=True))
        p_dec = (e_dec / jnp.sum(e_dec, axis=-1, keepdims=True)).astype(BF)
        c_dec = jnp.dot(p_dec, vcs[...], preferred_element_type=F32).astype(BF)
        for h in range(heads_local):
            dcs[:, pl.ds(h * HD, HD)] = c_dec[h * B:(h + 1) * B]
        dec_rows = pl.ds(mult(2 * RT + core * B, B), B)
        hops = (2, 1, 3, 0)
        srcs = (2, 3, 1)
        dx = [remote(dcs, ctxr.at[tp, dec_rows, :], dx_s.at[k], dx_r.at[k], side, at(hops[k])) for k in range(3)]
        for cp in dx:
            cp.start()
        ctxr[tp, dec_rows, :] = dcs[...]
        df_own = remote(dcs, ctxr.at[tp, dec_rows, :], df_s.at[3], df_r.at[3], partner, tp)
        df_own.start()

        got(1)
        kx[5].start()
        kx[3].start()
        got(2)
        kx[6].start()
        kx[4].start()

        df = []
        for k in range(3):
            ref = ctxr.at[at(srcs[k]), dec_rows, :]
            pltpu.make_async_copy(ref, ref, dx_r.at[k]).wait()
            df.append(remote(ref, ref, df_s.at[k], df_r.at[k], partner, tp))
            df[k].start()

        got(0)
        got(5)

        blks = [lax.rem(side + side_size - 2, side_size), lax.rem(side + side_size - 1, side_size), side]
        pre_rows = pl.ds(mult(core * RT, RT), RT)
        key_row = (side - 2) * R + lax.broadcasted_iota(jnp.int32, (1, 3 * R), 1)
        cx = []
        for k in range(4):
            r0 = mult(at(hops[k]) * RT, RT)
            q_row = side * R + r0 + lax.broadcasted_iota(jnp.int32, (RT, 1), 0)
            q_seg = seg_of(q_row)

            def head(h, c, k=k, r0=r0, q_row=q_row, q_seg=q_seg):
                q = qs[h, pl.ds(r0, RT), :]
                j = h // rep
                s = jnp.concatenate([lax.dot_general(q, kva[b, j], (((1,), (1,)), ((), ())), preferred_element_type=F32)
                                     for b in blks], axis=-1) * scale
                s = jnp.where((key_row >= q_seg) & (key_row <= q_row), s, -1e30)
                e = jnp.exp(s - jnp.max(s, axis=-1, keepdims=True))
                p = (e / jnp.sum(e, axis=-1, keepdims=True)).astype(BF)
                o = jnp.zeros((RT, HD), F32)
                for i, b in enumerate(blks):
                    o = o + jnp.dot(p[:, i * R:(i + 1) * R], kva[b, 2 + j], preferred_element_type=F32)
                cst[k, :, pl.ds(mult(h * HD, HD), HD)] = o.astype(BF)
                return c

            lax.fori_loop(0, heads_local, head, 0)
            if k < 3:
                cx.append(remote(cst.at[k], ctxr.at[tp, pre_rows, :], cx_s.at[k], cx_r.at[k], side, at(hops[k])))
                cx[k].start()
        ctxr[tp, pre_rows, :] = cst[3]
        cf = [None] * 4
        cf[3] = remote(cst.at[3], ctxr.at[tp, pre_rows, :], cf_s.at[3], cf_r.at[3], partner, tp)
        cf[3].start()
        for i in (3, 4):
            got(i)
            kx[i + 4].start()
        for k in range(3):
            ref = ctxr.at[at(srcs[k]), pre_rows, :]
            pltpu.make_async_copy(ref, ref, cx_r.at[k]).wait()
            cf[k] = remote(ref, ref, cf_s.at[k], cf_r.at[k], partner, tp)
            cf[k].start()

        p_pre = pl.ds(mult(oc * RT, RT), RT)
        p_dec_rows = pl.ds(mult(2 * RT + oc * B, B), B)
        for k in range(4):
            t = at(srcs[k]) if k < 3 else tp
            ref = ctxr.at[t, p_pre, :]
            pltpu.make_async_copy(ref, ref, cf_r.at[k]).wait()
            ref = ctxr.at[t, p_dec_rows, :]
            pltpu.make_async_copy(ref, ref, df_r.at[k]).wait()
        for cp in xres_l:
            cp.wait()
        for i, cp in enumerate(xres_r):
            cp.wait_send()
        ref = xres.at[p_pre, :]
        pltpu.make_async_copy(ref, ref, xr_r.at[0]).wait()
        ref = xres.at[p_dec_rows, :]
        pltpu.make_async_copy(ref, ref, xr_r.at[1]).wait()

        def h_copy(u):
            ref = hf.at[:, pl.ds(mult(core * DH + u * CW, CW), CW)]
            return remote(ref, ref, h_s.at[u], h_r.at[u], partner, tp)

        def out_proj(u, c):
            base = wo_base + u * Q
            slab_wait(mult(base, 256), Q, w_sem.at[n_kv + n_q + u])
            acc = jnp.zeros((M2, CW), F32)
            for t in range(tp_size):
                acc = acc + jnp.dot(ctxr[t], slab[pl.ds(mult(base + t * qw, 256), qw), :], preferred_element_type=F32)
            res = xres[:, pl.ds(mult(u * CW, CW), CW)].astype(F32)
            hf[:, pl.ds(mult(core * DH + u * CW, CW), CW)] = (res + acc.astype(BF).astype(F32)).astype(BF)
            h_copy(u).start()
            return c

        lax.fori_loop(0, n_o, out_proj, 0)
        n_early = gu_base // F
        for n in range(1, n_early):
            d_copy(n).start()
        for u in range(n_o):
            ref = hf.at[:, pl.ds(mult(oc * DH + u * CW, CW), CW)]
            pltpu.make_async_copy(ref, ref, h_r.at[u]).wait()

        def norm_h(i, c):
            r = pl.ds(mult(i * 32, 32), 32)
            hn[r, :] = norm(hf[r, :])
            return c

        lax.fori_loop(0, M2 // 32, norm_h, 0)

        def a_copy(j):
            ref = act.at[:, pl.ds(mult(core * FH + j * CW, CW), CW)]
            return remote(ref, ref, a_s.at[j], a_r.at[j], partner, tp)

        def last_slot(n):
            top = (n + 1) * F - gu_base
            slot = (top - 1) // (2 * D)
            return slot + ((n_g - 1 - slot) // GU_SLOTS) * GU_SLOTS

        def gate_up(j, c):
            slot = lax.rem(j, GU_SLOTS)
            base = mult(gu_base + slot * (2 * D), 256)
            slab_wait(base, 2 * D, g_sem.at[slot])
            g = jnp.dot(hn[...], slab[pl.ds(base, D), :], preferred_element_type=F32)
            u = jnp.dot(hn[...], slab[pl.ds(mult(base + D, 256), D), :], preferred_element_type=F32)
            g = g.astype(BF).astype(F32)
            u = u.astype(BF).astype(F32)
            act[:, pl.ds(mult(core * FH + j * CW, CW), CW)] = (g * jax.nn.sigmoid(g) * u).astype(BF)
            a_copy(j).start()

            @pl.when(j + GU_SLOTS < n_g)
            def _():
                start_gu(j + GU_SLOTS, slot)

            for n in range(n_early, n_d):
                @pl.when(j == last_slot(n))
                def _(n=n):
                    d_copy(n).start()
            return c

        lax.fori_loop(0, n_g, gate_up, 0)

        def a_got(j, c):
            ref = act.at[:, pl.ds(mult(oc * FH + j * CW, CW), CW)]
            pltpu.make_async_copy(ref, ref, a_r.at[j]).wait()
            return c

        lax.fori_loop(0, n_g, a_got, 0)

        up, down = at(1), at(tp_size - 1)
        own_out = pl.ds(mult(core * RT, RT), RT)
        his_out = pl.ds(mult(oc * RT, RT), RT)
        own_dec = pl.ds(mult(2 * RT + core * B, B), B)
        his_dec = pl.ds(mult(2 * RT + oc * B, B), B)
        rows_of = lambda t: pl.ds(mult(t * RT, RT), RT)

        def f_copies(n):
            cols = pl.ds(mult(core * DH + n * CW, CW), CW)
            there = hid.at[rows_of(tp), cols]
            mine, his = outst.at[n, own_out, :], outst.at[n, his_out, :]
            return [remote(mine, there, f_s.at[0, n], f_r.at[0, n], side, up),
                    remote(mine, there, f_s.at[1, n], f_r.at[1, n], side, down),
                    remote(his, there, f_s.at[2, n], f_r.at[2, n], partner, up),
                    remote(his, there, f_s.at[3, n], f_r.at[3, n], partner, down),
                    remote(his, there, f_s.at[4, n], f_r.at[4, n], partner, tp),
                    remote(outst.at[n, his_dec, :], decb.at[:, cols], f_s.at[5, n], f_r.at[5, n], partner, tp)]

        def down_proj(n, c):
            d_copy(n).wait()
            acc = jnp.dot(act[...], slab[pl.ds(mult(n * F, 256), F), :], preferred_element_type=F32)
            cols = pl.ds(mult(core * DH + n * CW, CW), CW)
            outst[n] = (hf[:, cols].astype(F32) + acc.astype(BF).astype(F32)).astype(BF)
            for cp in f_copies(n):
                cp.start()
            hid[rows_of(tp), cols] = outst[n, own_out, :]
            decb[:, cols] = outst[n, own_dec, :]
            return c

        lax.fori_loop(0, n_d, down_proj, 0)

        def piece(t, c_from, n):
            return hid.at[rows_of(t), pl.ds(mult(c_from * DH + n * CW, CW), CW)]

        def arrived(ref, sem):
            pltpu.make_async_copy(ref, ref, sem).wait()

        kind = {(0, 1): 0, (1, 1): 1, (0, 0): 2, (1, 0): 3}
        relays = []
        for n in range(n_d):
            for same in (1, 0):
                c_from = core if same else oc
                if n % 2 == 0:
                    ref = piece(down, c_from, n)
                    arrived(ref, f_r.at[kind[(0, same)], n])
                    cp = remote(ref, ref, r_s.at[same, n], r_r.at[same, n], side, up)
                else:
                    ref = piece(up, c_from, n)
                    arrived(ref, f_r.at[kind[(1, same)], n])
                    cp = remote(ref, ref, r_s.at[same, n], r_r.at[same, n], side, down)
                cp.start()
                relays.append(cp)

        for i in (6, 7, 8):
            got(i)
        start, length, total = jnp.int32(0), jnp.int32(0), jnp.int32(0)
        for r in range(nblk):
            mine = dst[r] == side
            start = start + jnp.where(mine, total, 0)
            length = length + jnp.where(mine, rl[r], 0)
            total = total + rl[r]
        o_row = lax.broadcasted_iota(jnp.int32, (PR, 1), 0)
        want = jnp.where(o_row // 2 < length, o_row // 2 + start, -1)
        col = lax.broadcasted_iota(jnp.int32, (1, 2 * R), 1)
        col_slot, col_row = col // R, lax.rem(col, R)
        code = want * 2 + lax.rem(o_row, 2)

        def install(b, c):
            kacc, vacc = c
            pick = jnp.where(code == (col_row + b * R) * 2 + col_slot, 1.0, 0.0).astype(BF)
            kk = kva[b, pl.ds(0, 2)].reshape(2 * R, HD)
            vv = kva[b, pl.ds(2, 2)].reshape(2 * R, HD)
            kps[...] = kps[...] + jnp.dot(pick, kk, preferred_element_type=F32).astype(BF)
            vps[...] = vps[...] + jnp.dot(pick, vv, preferred_element_type=F32).astype(BF)
            return c

        kps[...] = jnp.zeros((PR, HD), BF)
        vps[...] = jnp.zeros((PR, HD), BF)
        lax.fori_loop(0, nblk, install, (0, 0))
        outs = [pltpu.make_async_copy(kps, kp_o, o_sem.at[2]), pltpu.make_async_copy(vps, vp_o, o_sem.at[3])]
        for cp in outs:
            cp.start()

        def flush(t, i):
            r = rows_of(t)
            cp = pltpu.make_async_copy(hid.at[r, :], hid_o.at[r, :], o_sem.at[4 + i])
            cp.start()
            outs.append(cp)

        for n in range(n_d):
            arrived(piece(tp, oc, n), f_r.at[4, n])
            arrived(decb.at[:, pl.ds(mult(oc * DH + n * CW, CW), CW)], f_r.at[5, n])
        flush(tp, 0)
        cp = pltpu.make_async_copy(decb, dec_o, o_sem.at[8])
        cp.start()
        outs.append(cp)
        for n in range(n_d):
            for same in (1, 0):
                c_from = core if same else oc
                if n % 2 == 0:
                    arrived(piece(up, c_from, n), f_r.at[kind[(1, same)], n])
                else:
                    arrived(piece(down, c_from, n), f_r.at[kind[(0, same)], n])
        flush(up, 1)
        flush(down, 2)
        for n in range(n_d):
            for same in (1, 0):
                arrived(piece(at(2), core if same else oc, n), r_r.at[same, n])
        flush(at(2), 3)

        for cp in kx + dx + df + [df_own] + cx + cf + relays:
            cp.wait_send()

        def h_done(u, c):
            h_copy(u).wait_send()
            return c

        def a_done(j, c):
            a_copy(j).wait_send()
            return c

        def f_done(n, c):
            for cp in f_copies(n):
                cp.wait_send()
            return c

        lax.fori_loop(0, n_o, h_done, 0)
        lax.fori_loop(0, n_g, a_done, 0)
        lax.fori_loop(0, n_d, f_done, 0)
        kn_out.wait()
        vn_out.wait()
        for cp in outs:
            cp.wait()

    dma = lambda *s: pltpu.SemaphoreType.DMA(s)
    scratch = [
        pltpu.VMEM((slab_rows, CW), BF),
        pltpu.VMEM((R, D), BF), pltpu.VMEM((B, D), BF), pltpu.VMEM((M1, D), BF),
        pltpu.VMEM((n_kv + n_q, M1, CW), BF), pltpu.VMEM((heads_local, M1, HD), BF),
        pltpu.VMEM((nblk, 4, R, HD), BF), pltpu.VMEM((2 * B, 3 * HD), BF),
        pltpu.VMEM((CK, HD), BF), pltpu.VMEM((CK, HD), BF),
        pltpu.VMEM((M1, HD), F32), pltpu.VMEM((M1, HD), F32),
        pltpu.VMEM((B, qw), BF), pltpu.VMEM((4, RT, qw), BF), pltpu.VMEM((tp_size, M2, qw), BF),
        pltpu.VMEM((M2, DH), BF), pltpu.VMEM((M2, D), BF), pltpu.VMEM((M2, D), BF), pltpu.VMEM((M2, F), BF),
        pltpu.VMEM((n_d, M2, CW), BF), pltpu.VMEM((R, D), BF), pltpu.VMEM((B, D), BF),
        pltpu.VMEM((PR, HD), BF), pltpu.VMEM((PR, HD), BF),
        dma(6), dma(n_kv + n_q + n_o), dma(GU_SLOTS), dma(n_d),
        dma(2), dma(2), dma(9), dma(9), dma(3), dma(3), dma(4), dma(4),
        dma(3), dma(3), dma(4), dma(4), dma(n_o), dma(n_o), dma(n_g), dma(n_g),
        dma(6, n_d), dma(6, n_d), dma(2, n_d), dma(2, n_d), dma(9),
    ]
    return kernel, scratch, (R, D, B, PR, HD, CK)


def solution(mesh):
    tp_size = mesh.shape['tp']
    side_size = mesh.shape['side']
    rows_spec = P(('pair', 'side'), None)
    batch_spec = P(('pair', 'side'), None, None)
    cache_spec = P(('pair', 'side'), None, None, None, 'tp', None)
    prompt_spec = P(('pair', 'side'), None, None, 'tp', None)

    def local_step(x_loc, req_len, dest, w_qkv, w_out, w_gate, w_up, w_down, y_loc, kc_loc, vc_loc, clen_loc):
        R, D = x_loc.shape
        B, T, slots, HD = kc_loc.shape[2:]
        Q, F = w_out.shape[1], w_gate.shape[2]
        KV = (w_qkv.shape[2] - Q) // 2
        max_req = 2 * R - R // 4
        kernel, scratch, _ = make_kernel(tp_size, side_size, R, D, B, T, Q, KV, HD, F, max_req)
        half = HD // 2
        inv_freq = ROPE_BASE ** (-jnp.arange(half, dtype=F32) / half)
        one = jnp.ones((half,), F32)
        fq = jnp.zeros((8, HD), F32).at[0].set(jnp.concatenate([inv_freq, inv_freq])).at[1].set(jnp.concatenate([-one, one]))
        any_spec = pl.BlockSpec(memory_space=pl.ANY)
        smem = pl.BlockSpec(memory_space=pltpu.SMEM)
        CK = B * T * slots
        hid, dec, kp, vp, kn, vn = pl.pallas_call(
            kernel,
            name='prefill_decode',
            out_shape=[jax.ShapeDtypeStruct(s, BF) for s in
                       ((R, D), (B, D), (max_req * 2, HD), (max_req * 2, HD), (CK, HD), (CK, HD))],
            in_specs=[any_spec] * 9 + [smem] * 3 + [pl.BlockSpec(memory_space=pltpu.VMEM)],
            out_specs=[any_spec] * 6,
            scratch_shapes=scratch,
            compiler_params=pltpu.CompilerParams(collective_id=0, has_side_effects=True, vmem_limit_bytes=67043328),
        )(x_loc, y_loc[0], w_qkv[0], w_out[0], w_gate[0], w_up[0], w_down[0],
          kc_loc.reshape(CK, HD), vc_loc.reshape(CK, HD), req_len, dest, clen_loc[0], fq)
        cache = (1, 1, B, T, slots, HD)
        prompt = (1, 1, max_req, slots, HD)
        return hid, dec[None], kp.reshape(prompt), vp.reshape(prompt), kn.reshape(cache), vn.reshape(cache)

    return jax.shard_map(local_step, mesh=mesh,
                         in_specs=(rows_spec, P('pair'), P('pair'), P(), P(), P(), P(), P(), batch_spec, cache_spec, cache_spec, rows_spec),
                         out_specs=(rows_spec, batch_spec, prompt_spec, prompt_spec, cache_spec, cache_spec),
                         check_vma=False)
```

time: 1370 us -> 88.9 us (0.06)
  waiting for transfers between devices: 931 us -> 0 us
  other arithmetic: 182 us -> 0.09 us
  local copies, waits for them, and re-layouts: 156 us -> 14.1 us
  Pallas kernels: 0 us -> 73.8 us
  blocking collectives: 28.8 us -> 0 us
  matrix products: 24.4 us -> 0 us
  starting transfers between devices: 16.8 us -> 0 us
  between operations: 14.6 us -> 0.65 us
    all_gather x3 -> x0, waiting for transfers between devices: 909 us -> none  [the longest x1 792 us: local_step(): keys_full = lax.all_gather(keys_loc, 'tp', axis=2, tiled=True)]
    scatter x65 -> x0, other arithmetic: 170 us -> none
    pallas_call x0 -> x1, Pallas kernels: none -> 73.8 us  [local_step(): pl.pallas_call(kernel, name='prefill_decode', out_shape=[jax.ShapeDtypeSt...]
    unnamed x32 -> x6, local copies, waits for them, and re-layouts: 58.1 us -> 12.2 us
    psum x2 -> x0, blocking collectives: 28.8 us -> none  [the longest x1 15.3 us: finish_layer(): lax.psum(jnp.dot(context, wo_l, preferred_element_type=jnp.float32), 'tp')]
    slice x4 -> x0, local copies, waits for them, and re-layouts: 25.1 us -> none  [the longest x1 17 us: layer_weights(): qkv_l[:, :q_cols]]
    dot_general x8 -> x0, matrix products: 24.4 us -> none  [the longest x1 11.6 us: finish_layer(): jnp.dot(activated, wd_l, preferred_element_type=jnp.float32)]
    all_to_all x3 -> x0, waiting for transfers between devices: 20.8 us -> none  [the longest x1 20.8 us: local_step(): k_recv = lax.all_to_all(k_send, 'side', 0, 0, tiled=True)[0]]
  transfers between devices with their start and end apart: 6 -> 0, of which waited for: 4 -> 0; matrix products, arithmetic and copies ran while one was open for 21% -> 0% of each run, Pallas kernels for 0% -> 0%
where the time goes in v1:
time: 88.9 us; the launch traced here: 88.6 us
  Pallas kernels  73.8 us (83%)
  local copies, waits for them, and re-layouts  14.1 us (16%)
    pallas_call x1, Pallas kernels, local_step(): pl.pallas_call(kernel, name='prefill_decode', out_shape=[jax.ShapeDtypeSt...  73.8 us
    unnamed x6, local copies, waits for them, and re-layouts  12.2 us
    scatter x2, local copies, waits for them, and re-layouts, local_step(): jnp.zeros((8, HD), F32).at[0].set(jnp.concatenate([inv_freq, inv_freq]))  1.89 us

profile of v1, /device:TPU:97, one launch (start us, length us, event | category | flops | bytes accessed | tf_op | source)
XLA Modules:
  0.0 88.6 jit_solution(4884463603053641735)
XLA Ops:
  0.6 0.1 maximum_bitcast_fusion
  0.7 0.6 scatter.6
  1.3 1.3 %scatter.9.fq = f32[8,128]{1,0:T(8,128)} dynamic-update-slice(f32[8,128]{1,0:T(8,128)} %scatter.6, f32[1,128]{1,0:T(1,128)} %constant.62.clone.1, s32[]{:T(128)} %constant.63.clone.1, s32[]{:T(128)} %constant.64.clone.1) | dynamic-update-slice | bytes 1028 | tf_op jit(solution)/shard_map/scatter | solution.py:601
  2.6 73.8 %prefill_decode.1 = (bf16[256,3072]{1,0:T(8,128)(2,1)}, bf16[16,3072]{1,0:T(8,128)(2,1)}, bf16[896,128]{1,0:T(8,128)(2,1)}, bf16[896,128]{1,0:T(8,128)(2,1)}, bf...) custom-call(bf16[256,3072]{1,0:T(8,128)(2,1)} %x_h.1, bf16[16,3072]{1,0:T(8,128)(2,1)} %bitcast.27, ...), custom_call_target="tpu_custom_call" | custom-call | tf_op jit(solution)/shard_map/prefill_decode/pallas_call | solution.py:605
  76.4 2.7 %copy.25 = bf16[256,3072]{1,0:T(8,128)(2,1)} copy(bf16[256,3072]{1,0:T(8,128)(2,1)} %get-tuple-element.48) | data formatting | bytes 3145728
  79.0 1.5 %copy.26 = bf16[1,16,3072]{2,1,0:T(8,128)(2,1)} copy(bf16[1,16,3072]{2,1,0:T(8,128)(2,1)} %bitcast.28) | data formatting | bytes 196608
  80.6 1.8 %copy.27 = bf16[1,1,448,2,128]{4,3,2,1,0:T(2,128)(2,1)} copy(bf16[1,1,448,2,128]{4,3,2,1,0:T(2,128)(2,1)} %bitcast.26) | data formatting | bytes 458752
  82.4 1.8 %copy.28 = bf16[1,1,448,2,128]{4,3,2,1,0:T(2,128)(2,1)} copy(bf16[1,1,448,2,128]{4,3,2,1,0:T(2,128)(2,1)} %bitcast.25) | data formatting | bytes 458752
  84.1 2.2 %copy.29 = bf16[1,1,16,64,2,128]{5,4,3,2,1,0:T(2,128)(2,1)} copy(bf16[1,1,16,64,2,128]{5,4,3,2,1,0:T(2,128)(2,1)} %bitcast.24) | data formatting | bytes 1048576
  86.4 2.2 %copy.30 = bf16[1,1,16,64,2,128]{5,4,3,2,1,0:T(2,128)(2,1)} copy(bf16[1,1,16,64,2,128]{5,4,3,2,1,0:T(2,128)(2,1)} %bitcast.23) | data formatting | bytes 1048576
  (1 shorter events, 0.0 us)

commit v2 on v1

--- a/solution.py
+++ b/solution.py
@@ -1,5 +1,6 @@
 import jax
 import jax.numpy as jnp
+import numpy as np
 from jax import lax
 from jax.experimental import pallas as pl
 from jax.experimental.pallas import tpu as pltpu
@@ -10,7 +11,7 @@
 BF = jnp.bfloat16
 F32 = jnp.float32
 CW = 256
-GU_SLOTS = 8
+GU_SLOTS = 9
 MESH = pl.DeviceIdType.MESH
 
 
@@ -30,20 +31,23 @@
     M2 = 2 * RT + 2 * B
     n_kv, n_q = 2 * 2 * HD // CW, qw // CW
     n_o, n_g, n_d = DH // CW, FH // CW, DH // CW
-    wo_base = (n_kv + n_q) * D
+    wo_base = -(-(n_kv + n_q) * D // F) * F
     gu_base = wo_base + n_o * Q
     slab_rows = gu_base + GU_SLOTS * 2 * D
     CK = B * T * 2
     PR = max_req * 2
     scale = HD ** -0.5
+    n_first = wo_base // F
+    AB = D // CW
     nblk = side_size
 
     def kernel(x_h, y_h, wqkv_h, wo_h, wg_h, wu_h, wd_h, kc_h, vc_h, rl, dst, cl, fq,
                hid_o, dec_o, kp_o, vp_o, kn_o, vn_o,
-               slab, xs, ys, xn, raw, qs, kva, knv, kcs, vcs, cos_s, sin_s,
-               dcs, cst, ctxr, xres, hf, hn, act, outst, hid, decb, kps, vps,
+               slab, ub, ys, raw, qs, kva, knv, kcs, vcs, cos_s, sin_s,
+               dcs, cst, ctxr, xres, hf, hn, outst, hid, decb, kps, vps,
                in_sem, w_sem, g_sem, d_sem, xr_s, xr_r, kx_s, kx_r, cx_s, cx_r, cf_s, cf_r,
                dx_s, dx_r, df_s, df_r, h_s, h_r, a_s, a_r, f_s, f_r, r_s, r_r, o_sem):
+        xs, xn = ub.at[pl.ds(0, R), :], ub.at[pl.ds(R, M1), :]
         side = lax.axis_index('side')
         tp = lax.axis_index('tp')
         core = lax.rem(side, 2)
@@ -68,10 +72,8 @@
         vcol = [v_cols0 + tp * HD, v_cols0 + (tp + tp_size) * HD]
 
         def pieces(u):
-            if u == 0:
-                return [(kcol[0], 0, HD), (kcol[1], HD, HD)]
-            if u == 1:
-                return [(vcol[0], 0, HD), (vcol[1], HD, HD)]
+            if u < 2:
+                return [(kcol[u], 0, HD), (vcol[u], HD, HD)]
             lo, hi = (u - 2) * CW, (u - 1) * CW
             out = []
             for j in range(2):
@@ -165,8 +167,6 @@
         y_in.wait()
         xn[pl.ds(R, B), :] = norm(ys[...])
 
-        pl.semaphore_wait(barrier, len(peers))
-
         def remote(src, dst_ref, ss, rs, s, t):
             return pltpu.make_async_remote_copy(src_ref=src, dst_ref=dst_ref, send_sem=ss, recv_sem=rs,
                                                 device_id=dev(s, t), device_id_type=MESH)
@@ -176,8 +176,6 @@
                          xr_s.at[0], xr_r.at[0], partner, tp),
                   remote(y_h.at[:, pl.ds(his_cols, DH)], xres.at[pl.ds(mult(2 * RT + core * B, B), B), :],
                          xr_s.at[1], xr_r.at[1], partner, tp)]
-        for cp in xres_r:
-            cp.start()
 
         def project(u):
             w = slab[pl.ds(mult(u * D, 256), D), :]
@@ -194,38 +192,48 @@
 
         for u in range(n_o):
             start_wo(u)
-        lax.fori_loop(0, n_kv, project_loop, 0)
+
+        def blk(b, i0, n):
+            return kva.at[pl.ds(i0, n), pl.ds(mult(b * R, R), R), :]
+
+        plan = [(side, 0, 1, right, left), (side, 1, 1, right, left),
+                (side, 0, 1, partner, partner), (side, 1, 1, partner, partner),
+                (side, 0, 2, left, right),
+                (left, 0, 1, partner, p_left), (left, 1, 1, partner, p_left),
+                (left, 0, 1, right, far),
+                (right, 0, 2, partner, p_right), (right, 1, 1, left, far),
+                (far, 0, 1, partner, p_far), (far, 1, 1, partner, p_far)]
+        kx = [remote(blk(b, i0, n), blk(b, i0, n), kx_s.at[i], kx_r.at[i], to, tp)
+              for i, (b, i0, n, to, _) in enumerate(plan)]
+
+        def got(i):
+            ref = blk(plan[i][4], plan[i][1], plan[i][2])
+            pltpu.make_async_copy(ref, ref, kx_r.at[i]).wait()
+
+        own_rows = pl.ds(mult(side * R, R), R)
         for j in range(2):
-            k_j = rope(raw[0, :, pl.ds(j * HD, HD)])
-            kva[side, j] = k_j[:R]
+            slab_wait(j * D, D, w_sem.at[j])
+            project(j)
+            k_j = rope(raw[j, :, pl.ds(0, HD)])
+            v_j = raw[j, :, pl.ds(HD, HD)]
+            kva[j, own_rows, pl.ds(0, HD)] = k_j[:R]
+            kva[j, own_rows, pl.ds(HD, HD)] = v_j[:R]
+            if j == 0:
+                pl.semaphore_wait(barrier, len(peers))
+            kx[j].start()
+            kx[2 + j].start()
             knv[pl.ds(j * B, B), pl.ds(0, HD)] = k_j[R:]
-            v_j = raw[1, :, pl.ds(j * HD, HD)]
-            kva[side, 2 + j] = v_j[:R]
             knv[pl.ds(j * B, B), pl.ds(HD, HD)] = v_j[R:]
+        kx[4].start()
+        for cp in xres_r:
+            cp.start()
         knv[:, pl.ds(2 * HD, HD)] = jnp.ones((2 * B, HD), BF)
-
-        lo, hi = pl.ds(0, 2), pl.ds(2, 2)
-        kx = [remote(kva.at[side], kva.at[side], kx_s.at[0], kx_r.at[0], partner, tp),
-              remote(kva.at[side], kva.at[side], kx_s.at[1], kx_r.at[1], right, tp),
-              remote(kva.at[side], kva.at[side], kx_s.at[2], kx_r.at[2], left, tp),
-              remote(kva.at[left, lo], kva.at[left, lo], kx_s.at[3], kx_r.at[3], right, tp),
-              remote(kva.at[right, hi], kva.at[right, hi], kx_s.at[4], kx_r.at[4], left, tp),
-              remote(kva.at[left], kva.at[left], kx_s.at[5], kx_r.at[5], partner, tp),
-              remote(kva.at[right], kva.at[right], kx_s.at[6], kx_r.at[6], partner, tp),
-              remote(kva.at[far, lo], kva.at[far, lo], kx_s.at[7], kx_r.at[7], partner, tp),
-              remote(kva.at[far, hi], kva.at[far, hi], kx_s.at[8], kx_r.at[8], partner, tp)]
-        for i in (1, 0, 2):
-            kx[i].start()
-
-        def got(i):
-            blk = (partner, left, right, far, far, p_left, p_right, p_far, p_far)[i]
-            ref = kva.at[blk, lo] if i in (3, 7) else kva.at[blk, hi] if i in (4, 8) else kva.at[blk]
-            pltpu.make_async_copy(ref, ref, kx_r.at[i]).wait()
 
         lax.fori_loop(n_kv, n_kv + n_q, project_loop, 0)
         for slot in range(GU_SLOTS):
             start_gu(slot, slot)
-        d_copy(0).start()
+        for n in range(n_first):
+            d_copy(n).start()
         for h in range(heads_local):
             u, off = divmod(h * HD, CW)
             qs[h] = rope(raw[2 + u, :, pl.ds(off, HD)])
@@ -283,69 +291,86 @@
         df_own = remote(dcs, ctxr.at[tp, dec_rows, :], df_s.at[3], df_r.at[3], partner, tp)
         df_own.start()
 
-        got(1)
+        got(0)
         kx[5].start()
-        kx[3].start()
+        kx[7].start()
+
         got(2)
-        kx[6].start()
-        kx[4].start()
-
-        df = []
-        for k in range(3):
-            ref = ctxr.at[at(srcs[k]), dec_rows, :]
-            pltpu.make_async_copy(ref, ref, dx_r.at[k]).wait()
-            df.append(remote(ref, ref, df_s.at[k], df_r.at[k], partner, tp))
-            df[k].start()
-
-        got(0)
         got(5)
 
         blks = [lax.rem(side + side_size - 2, side_size), lax.rem(side + side_size - 1, side_size), side]
         pre_rows = pl.ds(mult(core * RT, RT), RT)
         key_row = (side - 2) * R + lax.broadcasted_iota(jnp.int32, (1, 3 * R), 1)
-        cx = []
-        for k in range(4):
+        QR = rep * RT
+        q_off = lax.rem(lax.broadcasted_iota(jnp.int32, (QR, 1), 0), RT)
+
+        def attend(j, k):
             r0 = mult(at(hops[k]) * RT, RT)
-            q_row = side * R + r0 + lax.broadcasted_iota(jnp.int32, (RT, 1), 0)
+            q_row = side * R + r0 + q_off
             q_seg = seg_of(q_row)
-
-            def head(h, c, k=k, r0=r0, q_row=q_row, q_seg=q_seg):
-                q = qs[h, pl.ds(r0, RT), :]
-                j = h // rep
-                s = jnp.concatenate([lax.dot_general(q, kva[b, j], (((1,), (1,)), ((), ())), preferred_element_type=F32)
-                                     for b in blks], axis=-1) * scale
-                s = jnp.where((key_row >= q_seg) & (key_row <= q_row), s, -1e30)
-                e = jnp.exp(s - jnp.max(s, axis=-1, keepdims=True))
-                p = (e / jnp.sum(e, axis=-1, keepdims=True)).astype(BF)
-                o = jnp.zeros((RT, HD), F32)
-                for i, b in enumerate(blks):
-                    o = o + jnp.dot(p[:, i * R:(i + 1) * R], kva[b, 2 + j], preferred_element_type=F32)
-                cst[k, :, pl.ds(mult(h * HD, HD), HD)] = o.astype(BF)
-                return c
-
-            lax.fori_loop(0, heads_local, head, 0)
-            if k < 3:
-                cx.append(remote(cst.at[k], ctxr.at[tp, pre_rows, :], cx_s.at[k], cx_r.at[k], side, at(hops[k])))
-                cx[k].start()
-        ctxr[tp, pre_rows, :] = cst[3]
-        cf = [None] * 4
-        cf[3] = remote(cst.at[3], ctxr.at[tp, pre_rows, :], cf_s.at[3], cf_r.at[3], partner, tp)
-        cf[3].start()
-        for i in (3, 4):
-            got(i)
-            kx[i + 4].start()
+            q = qs[pl.ds(j * rep, rep), pl.ds(r0, RT), :].reshape(QR, HD)
+            held = lambda i, b: kva[j, pl.ds(mult(b * R, R), R), pl.ds(i * HD, HD)]
+            s = jnp.concatenate([lax.dot_general(q, held(0, b), (((1,), (1,)), ((), ())), preferred_element_type=F32)
+                                 for b in blks], axis=-1) * scale
+            s = jnp.where((key_row >= q_seg) & (key_row <= q_row), s, -1e30)
+            e = jnp.exp(s - jnp.max(s, axis=-1, keepdims=True))
+            p = (e * (1.0 / jnp.sum(e, axis=-1, keepdims=True))).astype(BF)
+            o = jnp.zeros((QR, HD), F32)
+            for i, b in enumerate(blks):
+                o = o + jnp.dot(p[:, i * R:(i + 1) * R], held(1, b), preferred_element_type=F32)
+            o = o.astype(BF)
+            for h in range(rep):
+                cst[j, k, :, pl.ds(h * HD, HD)] = o[h * RT:(h + 1) * RT]
+
+        def ctx_at(t, rows_, j):
+            return ctxr.at[t, rows_, pl.ds(j * hw, hw)]
+
+        cx = [[remote(cst.at[j, k], ctx_at(tp, pre_rows, j), cx_s.at[j, k], cx_r.at[j, k], side, at(hops[k]))
+               for k in range(3)] for j in range(2)]
+        cf = [[remote(ctx_at(at(srcs[k]), pre_rows, j), ctx_at(at(srcs[k]), pre_rows, j), cf_s.at[j, k], cf_r.at[j, k], partner, tp)
+               for k in range(3)] + [remote(cst.at[j, 3], ctx_at(tp, pre_rows, j), cf_s.at[j, 3], cf_r.at[j, 3], partner, tp)]
+              for j in range(2)]
+
+        def pass_ctx(j, k):
+            ref = ctx_at(at(srcs[k]), pre_rows, j)
+            pltpu.make_async_copy(ref, ref, cx_r.at[j, k]).wait()
+            cf[j][k].start()
+
+        df = []
+        for j in range(2):
+            for k in range(4):
+                attend(j, k)
+                if k < 3:
+                    cx[j][k].start()
+                else:
+                    ctxr[tp, pre_rows, pl.ds(j * hw, hw)] = cst[j, 3]
+                    cf[j][3].start()
+                if j == 0 and k == 2:
+                    got(1)
+                    kx[6].start()
+                if j == 1 and k > 0:
+                    pass_ctx(0, k - 1)
+            if j == 0:
+                for k in range(3):
+                    ref = ctxr.at[at(srcs[k]), dec_rows, :]
+                    pltpu.make_async_copy(ref, ref, dx_r.at[k]).wait()
+                    df.append(remote(ref, ref, df_s.at[k], df_r.at[k], partner, tp))
+                    df[k].start()
+                got(3)
+                got(6)
+                got(4)
+                kx[8].start()
+                kx[9].start()
+
         for k in range(3):
-            ref = ctxr.at[at(srcs[k]), pre_rows, :]
-            pltpu.make_async_copy(ref, ref, cx_r.at[k]).wait()
-            cf[k] = remote(ref, ref, cf_s.at[k], cf_r.at[k], partner, tp)
-            cf[k].start()
-
+            pass_ctx(1, k)
         p_pre = pl.ds(mult(oc * RT, RT), RT)
         p_dec_rows = pl.ds(mult(2 * RT + oc * B, B), B)
         for k in range(4):
             t = at(srcs[k]) if k < 3 else tp
-            ref = ctxr.at[t, p_pre, :]
-            pltpu.make_async_copy(ref, ref, cf_r.at[k]).wait()
+            for j in range(2):
+                ref = ctx_at(t, p_pre, j)
+                pltpu.make_async_copy(ref, ref, cf_r.at[j, k]).wait()
             ref = ctxr.at[t, p_dec_rows, :]
             pltpu.make_async_copy(ref, ref, df_r.at[k]).wait()
         for cp in xres_l:
@@ -373,9 +398,10 @@
             return c
 
         lax.fori_loop(0, n_o, out_proj, 0)
-        n_early = gu_base // F
-        for n in range(1, n_early):
-            d_copy(n).start()
+        for i in (7, 9):
+            got(i)
+        kx[10].start()
+        kx[11].start()
         for u in range(n_o):
             ref = hf.at[:, pl.ds(mult(oc * DH + u * CW, CW), CW)]
             pltpu.make_async_copy(ref, ref, h_r.at[u]).wait()
@@ -387,12 +413,18 @@
 
         lax.fori_loop(0, M2 // 32, norm_h, 0)
 
+        def act_at(c_of, j):
+            g = c_of * n_g + j
+            return ub.at[pl.ds(mult((g // AB) * M2, 16), M2), pl.ds(mult(lax.rem(g, AB) * CW, CW), CW)]
+
         def a_copy(j):
-            ref = act.at[:, pl.ds(mult(core * FH + j * CW, CW), CW)]
+            ref = act_at(core, j)
             return remote(ref, ref, a_s.at[j], a_r.at[j], partner, tp)
 
         def last_slot(n):
             top = (n + 1) * F - gu_base
+            if top <= 0:
+                return 2 * (n - n_first) + 2
             slot = (top - 1) // (2 * D)
             return slot + ((n_g - 1 - slot) // GU_SLOTS) * GU_SLOTS
 
@@ -404,14 +436,14 @@
             u = jnp.dot(hn[...], slab[pl.ds(mult(base + D, 256), D), :], preferred_element_type=F32)
             g = g.astype(BF).astype(F32)
             u = u.astype(BF).astype(F32)
-            act[:, pl.ds(mult(core * FH + j * CW, CW), CW)] = (g * jax.nn.sigmoid(g) * u).astype(BF)
+            act_at(core, j)[...] = (g * jax.nn.sigmoid(g) * u).astype(BF)
             a_copy(j).start()
 
             @pl.when(j + GU_SLOTS < n_g)
             def _():
                 start_gu(j + GU_SLOTS, slot)
 
-            for n in range(n_early, n_d):
+            for n in range(n_first, n_d):
                 @pl.when(j == last_slot(n))
                 def _(n=n):
                     d_copy(n).start()
@@ -420,7 +452,7 @@
         lax.fori_loop(0, n_g, gate_up, 0)
 
         def a_got(j, c):
-            ref = act.at[:, pl.ds(mult(oc * FH + j * CW, CW), CW)]
+            ref = act_at(oc, j)
             pltpu.make_async_copy(ref, ref, a_r.at[j]).wait()
             return c
 
@@ -446,7 +478,11 @@
 
         def down_proj(n, c):
             d_copy(n).wait()
-            acc = jnp.dot(act[...], slab[pl.ds(mult(n * F, 256), F), :], preferred_element_type=F32)
+            acc = jnp.zeros((M2, CW), F32)
+            for i in range(-(-F // D)):
+                w = min(D, F - i * D)
+                acc = acc + jnp.dot(ub[pl.ds(i * M2, M2), pl.ds(0, w)], slab[pl.ds(mult(n * F + i * D, 256), w), :],
+                                    preferred_element_type=F32)
             cols = pl.ds(mult(core * DH + n * CW, CW), CW)
             outst[n] = (hf[:, cols].astype(F32) + acc.astype(BF).astype(F32)).astype(BF)
             for cp in f_copies(n):
@@ -479,7 +515,7 @@
                 cp.start()
                 relays.append(cp)
 
-        for i in (6, 7, 8):
+        for i in (8, 10, 11):
             got(i)
         start, length, total = jnp.int32(0), jnp.int32(0), jnp.int32(0)
         for r in range(nblk):
@@ -487,24 +523,20 @@
             start = start + jnp.where(mine, total, 0)
             length = length + jnp.where(mine, rl[r], 0)
             total = total + rl[r]
-        o_row = lax.broadcasted_iota(jnp.int32, (PR, 1), 0)
-        want = jnp.where(o_row // 2 < length, o_row // 2 + start, -1)
-        col = lax.broadcasted_iota(jnp.int32, (1, 2 * R), 1)
-        col_slot, col_row = col // R, lax.rem(col, R)
-        code = want * 2 + lax.rem(o_row, 2)
-
-        def install(b, c):
-            kacc, vacc = c
-            pick = jnp.where(code == (col_row + b * R) * 2 + col_slot, 1.0, 0.0).astype(BF)
-            kk = kva[b, pl.ds(0, 2)].reshape(2 * R, HD)
-            vv = kva[b, pl.ds(2, 2)].reshape(2 * R, HD)
-            kps[...] = kps[...] + jnp.dot(pick, kk, preferred_element_type=F32).astype(BF)
-            vps[...] = vps[...] + jnp.dot(pick, vv, preferred_element_type=F32).astype(BF)
-            return c
-
-        kps[...] = jnp.zeros((PR, HD), BF)
-        vps[...] = jnp.zeros((PR, HD), BF)
-        lax.fori_loop(0, nblk, install, (0, 0))
+        IR = 128
+        col = lax.broadcasted_iota(jnp.int32, (1, 2 * nblk * R), 1)
+
+        def install(i, c):
+            r = pl.ds(mult(i * IR, IR), IR)
+            o_row = lax.broadcasted_iota(jnp.int32, (IR, 1), 0) + i * IR
+            code = jnp.where(o_row // 2 < length, o_row // 2 + start + lax.rem(o_row, 2) * (nblk * R), -1)
+            pick = jnp.where(code == col, 1.0, 0.0).astype(BF)
+            out = jnp.dot(pick, kva[...].reshape(2 * nblk * R, 2 * HD), preferred_element_type=F32).astype(BF)
+            kps[r, :] = out[:, :HD]
+            vps[r, :] = out[:, HD:]
+            return c
+
+        lax.fori_loop(0, PR // IR, install, 0)
         outs = [pltpu.make_async_copy(kps, kp_o, o_sem.at[2]), pltpu.make_async_copy(vps, vp_o, o_sem.at[3])]
         for cp in outs:
             cp.start()
@@ -536,7 +568,7 @@
                 arrived(piece(at(2), core if same else oc, n), r_r.at[same, n])
         flush(at(2), 3)
 
-        for cp in kx + dx + df + [df_own] + cx + cf + relays:
+        for cp in kx + dx + df + [df_own] + cx[0] + cx[1] + cf[0] + cf[1] + relays:
             cp.wait_send()
 
         def h_done(u, c):
@@ -563,21 +595,56 @@
     dma = lambda *s: pltpu.SemaphoreType.DMA(s)
     scratch = [
         pltpu.VMEM((slab_rows, CW), BF),
-        pltpu.VMEM((R, D), BF), pltpu.VMEM((B, D), BF), pltpu.VMEM((M1, D), BF),
+        pltpu.VMEM((max(R + M1, -(-F // D) * M2), D), BF), pltpu.VMEM((B, D), BF),
         pltpu.VMEM((n_kv + n_q, M1, CW), BF), pltpu.VMEM((heads_local, M1, HD), BF),
-        pltpu.VMEM((nblk, 4, R, HD), BF), pltpu.VMEM((2 * B, 3 * HD), BF),
+        pltpu.VMEM((2, nblk * R, 2 * HD), BF), pltpu.VMEM((2 * B, 3 * HD), BF),
         pltpu.VMEM((CK, HD), BF), pltpu.VMEM((CK, HD), BF),
         pltpu.VMEM((M1, HD), F32), pltpu.VMEM((M1, HD), F32),
-        pltpu.VMEM((B, qw), BF), pltpu.VMEM((4, RT, qw), BF), pltpu.VMEM((tp_size, M2, qw), BF),
-        pltpu.VMEM((M2, DH), BF), pltpu.VMEM((M2, D), BF), pltpu.VMEM((M2, D), BF), pltpu.VMEM((M2, F), BF),
+        pltpu.VMEM((B, qw), BF), pltpu.VMEM((2, 4, RT, hw), BF), pltpu.VMEM((tp_size, M2, qw), BF),
+        pltpu.VMEM((M2, DH), BF), pltpu.VMEM((M2, D), BF), pltpu.VMEM((M2, D), BF),
         pltpu.VMEM((n_d, M2, CW), BF), pltpu.VMEM((R, D), BF), pltpu.VMEM((B, D), BF),
         pltpu.VMEM((PR, HD), BF), pltpu.VMEM((PR, HD), BF),
         dma(6), dma(n_kv + n_q + n_o), dma(GU_SLOTS), dma(n_d),
-        dma(2), dma(2), dma(9), dma(9), dma(3), dma(3), dma(4), dma(4),
+        dma(2), dma(2), dma(12), dma(12), dma(2, 3), dma(2, 3), dma(2, 4), dma(2, 4),
         dma(3), dma(3), dma(4), dma(4), dma(n_o), dma(n_o), dma(n_g), dma(n_g),
         dma(6, n_d), dma(6, n_d), dma(2, n_d), dma(2, n_d), dma(9),
     ]
     return kernel, scratch, (R, D, B, PR, HD, CK)
+
+
+def write_out(*arrays):
+    n = len(arrays)
+    cuts = []
+    for i, a in enumerate(arrays):
+        parts = 4 if i == 0 else 1
+        step = a.shape[0] // parts
+        cuts += [(i, p * step, step) for p in range(parts)]
+
+    def kernel(*refs):
+        ins, outs, bufs, sem_in, sem_out = refs[:n], refs[n:2 * n], refs[2 * n:3 * n], refs[3 * n], refs[3 * n + 1]
+        reads = [pltpu.make_async_copy(ins[i].at[pl.ds(r, w), :], bufs[i].at[pl.ds(r, w), :], sem_in.at[k])
+                 for k, (i, r, w) in enumerate(cuts)]
+        writes = [pltpu.make_async_copy(bufs[i].at[pl.ds(r, w), :], outs[i].at[pl.ds(r, w), :], sem_out.at[k])
+                  for k, (i, r, w) in enumerate(cuts)]
+        for cp in reads:
+            cp.start()
+        for rd, wr in zip(reads, writes):
+            rd.wait()
+            wr.start()
+        for wr in writes:
+            wr.wait()
+
+    any_spec = pl.BlockSpec(memory_space=pl.ANY)
+    return pl.pallas_call(
+        kernel,
+        name='write_out',
+        out_shape=[jax.ShapeDtypeStruct(a.shape, a.dtype) for a in arrays],
+        in_specs=[any_spec] * n,
+        out_specs=[any_spec] * n,
+        scratch_shapes=[pltpu.VMEM(a.shape, a.dtype) for a in arrays]
+        + [pltpu.SemaphoreType.DMA((len(cuts),)), pltpu.SemaphoreType.DMA((len(cuts),))],
+        compiler_params=pltpu.CompilerParams(vmem_limit_bytes=67043328),
+    )(*arrays)
 
 
 def solution(mesh):
@@ -596,9 +663,11 @@
         max_req = 2 * R - R // 4
         kernel, scratch, _ = make_kernel(tp_size, side_size, R, D, B, T, Q, KV, HD, F, max_req)
         half = HD // 2
-        inv_freq = ROPE_BASE ** (-jnp.arange(half, dtype=F32) / half)
-        one = jnp.ones((half,), F32)
-        fq = jnp.zeros((8, HD), F32).at[0].set(jnp.concatenate([inv_freq, inv_freq])).at[1].set(jnp.concatenate([-one, one]))
+        inv_freq = np.float32(ROPE_BASE) ** (-np.arange(half, dtype=np.float32) / np.float32(half))
+        table = np.zeros((8, HD), np.float32)
+        table[0] = np.concatenate([inv_freq, inv_freq])
+        table[1] = np.concatenate([-np.ones(half), np.ones(half)])
+        fq = jnp.asarray(table)
         any_spec = pl.BlockSpec(memory_space=pl.ANY)
         smem = pl.BlockSpec(memory_space=pltpu.SMEM)
         CK = B * T * slots
@@ -613,6 +682,7 @@
             compiler_params=pltpu.CompilerParams(collective_id=0, has_side_effects=True, vmem_limit_bytes=67043328),
         )(x_loc, y_loc[0], w_qkv[0], w_out[0], w_gate[0], w_up[0], w_down[0],
           kc_loc.reshape(CK, HD), vc_loc.reshape(CK, HD), req_len, dest, clen_loc[0], fq)
+        hid, dec, kp, vp, kn, vn = write_out(hid, dec, kp, vp, kn, vn)
         cache = (1, 1, B, T, slots, HD)
         prompt = (1, 1, max_req, slots, HD)
         return hid, dec[None], kp.reshape(prompt), vp.reshape(prompt), kn.reshape(cache), vn.reshape(cache)

time: 88.9 us -> 67.6 us (0.76)
  local copies, waits for them, and re-layouts: 14.1 us -> 0 us
  Pallas kernels: 73.8 us -> 66.8 us
    unnamed x6 -> x0, local copies, waits for them, and re-layouts: 12.2 us -> none
    pallas_call x1, Pallas kernels: 73.8 us -> 64 us  [local_step(): pl.pallas_call(kernel, name='prefill_decode', out_shape=[jax.ShapeDtypeSt...]
    pallas_call x0 -> x1, Pallas kernels: none -> 2.82 us  [write_out(): pl.pallas_call(kernel, name='write_out', out_shape=[jax.ShapeDtypeStruct(...]
    scatter x2 -> x0, local copies, waits for them, and re-layouts: 1.89 us -> none  [local_step(): jnp.zeros((8, HD), F32).at[0].set(jnp.concatenate([inv_freq, inv_freq]))]
where the time goes in v2:
time: 67.6 us; the launch traced here: 67.5 us
  Pallas kernels  66.8 us (99%)
    pallas_call x1, Pallas kernels, local_step(): pl.pallas_call(kernel, name='prefill_decode', out_shape=[jax.ShapeDtypeSt...  64 us
    pallas_call x1, Pallas kernels, write_out(): pl.pallas_call(kernel, name='write_out', out_shape=[jax.ShapeDtypeStruct(...  2.82 us

profile of v2, /device:TPU:97, one launch (start us, length us, event | category | flops | bytes accessed | tf_op | source)
XLA Modules:
  0.0 67.5 jit_solution(6212107267052252967)
XLA Ops:
  0.6 64.0 %prefill_decode.1 = (bf16[256,3072]{1,0:T(8,128)(2,1)}, bf16[16,3072]{1,0:T(8,128)(2,1)}, bf16[896,128]{1,0:T(8,128)(2,1)}, bf16[896,128]{1,0:T(8,128)(2,1)}, bf...) custom-call(bf16[256,3072]{1,0:T(8,128)(2,1)} %x_h.1, bf16[16,3072]{1,0:T(8,128)(2,1)} %bitcast.21, ...), custom_call_target="tpu_custom_call" | custom-call | tf_op jit(solution)/shard_map/prefill_decode/pallas_call | solution.py:674
  64.6 2.8 %write_out.1 = (bf16[256,3072]{1,0:T(8,128)(2,1)}, bf16[16,3072]{1,0:T(8,128)(2,1)}, bf16[896,128]{1,0:T(8,128)(2,1)}, bf16[896,128]{1,0:T(8,128)(2,1)}, bf16[20...) custom-call(bf16[256,3072]{1,0:T(8,128)(2,1)} %get-tuple-element.18.refs_0_, bf16[16,3072]{1,0:T(8,128)(2,1)} %get-tuple-element.19.refs_1_, ...), custom_call_target="tpu_custom_call" | custom-call | tf_op jit(solution)/shard_map/write_out/pallas_call | solution.py:638

commit v3 on v2

--- a/solution.py
+++ b/solution.py
@@ -37,13 +37,14 @@
     CK = B * T * 2
     PR = max_req * 2
     scale = HD ** -0.5
+    WK = max_req + RT
     n_first = wo_base // F
     AB = D // CW
     nblk = side_size
 
-    def kernel(x_h, y_h, wqkv_h, wo_h, wg_h, wu_h, wd_h, kc_h, vc_h, rl, dst, cl, fq,
+    def kernel(x_h, y_h, wqkv_h, wo_h, wg_h, wu_h, wd_h, kc_h, vc_h, rl_h, dst_h, cl_h, fq_h,
                hid_o, dec_o, kp_o, vp_o, kn_o, vn_o,
-               slab, ub, ys, raw, qs, kva, knv, kcs, vcs, cos_s, sin_s,
+               rl, dst, cl, fq, slab, ub, ys, raw, qs, kva, knv, kcs, vcs, cos_s, sin_s, bias_s,
                dcs, cst, ctxr, xres, hf, hn, outst, hid, decb, kps, vps,
                in_sem, w_sem, g_sem, d_sem, xr_s, xr_r, kx_s, kx_r, cx_s, cx_r, cf_s, cf_r,
                dx_s, dx_r, df_s, df_r, h_s, h_r, a_s, a_r, f_s, f_r, r_s, r_r, o_sem):
@@ -92,11 +93,8 @@
 
         def start_wo(u):
             col = mult(core * DH + u * CW, 128)
-            for t in range(tp_size):
-                for j in range(2):
-                    pltpu.make_async_copy(wo_h.at[pl.ds((t + j * tp_size) * hw, hw), pl.ds(col, CW)],
-                                          slab.at[pl.ds(wo_base + u * Q + t * qw + j * hw, hw), :],
-                                          w_sem.at[n_kv + n_q + u]).start()
+            pltpu.make_async_copy(wo_h.at[:, pl.ds(col, CW)], slab.at[pl.ds(wo_base + u * Q, Q), :],
+                                  w_sem.at[n_kv + n_q + u]).start()
 
         def start_gu(j, slot):
             col = mult(core * FH + j * CW, 128)
@@ -108,10 +106,14 @@
             return pltpu.make_async_copy(wd_h.at[:, pl.ds(mult(core * DH + n * CW, 128), CW)],
                                          slab.at[pl.ds(mult(n * F, 256), F), :], d_sem.at[n])
 
-        x_in = pltpu.make_async_copy(x_h, xs, in_sem.at[0])
+        small = [pltpu.make_async_copy(a, b, in_sem.at[6 + i])
+                 for i, (a, b) in enumerate(((rl_h, rl), (dst_h, dst), (cl_h, cl), (fq_h, fq)))]
+        XC = 4
+        x_in = [pltpu.make_async_copy(x_h.at[pl.ds(i * (R // XC), R // XC), :], xs.at[pl.ds(i * (R // XC), R // XC), :],
+                                      in_sem.at[10 + i]) for i in range(XC)]
         y_in = pltpu.make_async_copy(y_h, ys, in_sem.at[1])
-        x_in.start()
-        y_in.start()
+        for cp in small + x_in + [y_in]:
+            cp.start()
         for u in range(n_kv + n_q):
             start_qkv(u)
 
@@ -142,6 +144,8 @@
                 seg = jnp.where(rows >= total, total, seg)
             return seg
 
+        for cp in small:
+            cp.wait()
         idx = lax.broadcasted_iota(jnp.int32, (M1, 1), 0)
         rows = idx + side * R
         pos = rows - seg_of(rows)
@@ -156,14 +160,15 @@
             sc = lax.rsqrt(jnp.sum(w * w, axis=-1, keepdims=True) / D + NORM_EPS)
             return (w * sc).astype(BF)
 
-        x_in.wait()
-
-        def norm_x(i, c):
-            r = pl.ds(mult(i * 32, 32), 32)
-            xn[r, :] = norm(xs[r, :])
-            return c
-
-        lax.fori_loop(0, R // 32, norm_x, 0)
+        for i in range(XC):
+            x_in[i].wait()
+
+            def norm_x(k, c, i=i):
+                r = pl.ds(mult(i * (R // XC) + k * 32, 32), 32)
+                xn[r, :] = norm(xs[r, :])
+                return c
+
+            lax.fori_loop(0, R // XC // 32, norm_x, 0, unroll=True)
         y_in.wait()
         xn[pl.ds(R, B), :] = norm(ys[...])
 
@@ -184,11 +189,6 @@
         def rope(v):
             w = v.astype(F32)
             return (w * cos_s[...] + pltpu.roll(w, HD // 2, 1) * sin_s[...]).astype(BF)
-
-        def project_loop(i, c):
-            slab_wait(mult(i * D, 256), D, w_sem.at[i])
-            project(i)
-            return c
 
         for u in range(n_o):
             start_wo(u)
@@ -211,25 +211,37 @@
             pltpu.make_async_copy(ref, ref, kx_r.at[i]).wait()
 
         own_rows = pl.ds(mult(side * R, R), R)
-        for j in range(2):
-            slab_wait(j * D, D, w_sem.at[j])
+        pl.semaphore_wait(barrier, len(peers))
+
+        def keys_values(j, c):
+            slab_wait(mult(j * D, 256), D, w_sem.at[j])
             project(j)
             k_j = rope(raw[j, :, pl.ds(0, HD)])
             v_j = raw[j, :, pl.ds(HD, HD)]
             kva[j, own_rows, pl.ds(0, HD)] = k_j[:R]
             kva[j, own_rows, pl.ds(HD, HD)] = v_j[:R]
-            if j == 0:
-                pl.semaphore_wait(barrier, len(peers))
-            kx[j].start()
-            kx[2 + j].start()
-            knv[pl.ds(j * B, B), pl.ds(0, HD)] = k_j[R:]
-            knv[pl.ds(j * B, B), pl.ds(HD, HD)] = v_j[R:]
+            ref = blk(side, j, 1)
+            remote(ref, ref, kx_s.at[j], kx_r.at[j], right, tp).start()
+            remote(ref, ref, kx_s.at[2 + j], kx_r.at[2 + j], partner, tp).start()
+            knv[pl.ds(mult(j * B, B), B), pl.ds(0, HD)] = k_j[R:]
+            knv[pl.ds(mult(j * B, B), B), pl.ds(HD, HD)] = v_j[R:]
+            return c
+
+        lax.fori_loop(0, 2, keys_values, 0)
         kx[4].start()
         for cp in xres_r:
             cp.start()
         knv[:, pl.ds(2 * HD, HD)] = jnp.ones((2 * B, HD), BF)
 
-        lax.fori_loop(n_kv, n_kv + n_q, project_loop, 0)
+        for u in range(n_kv, n_kv + n_q):
+            slab_wait(u * D, D, w_sem.at[u])
+
+        def queries(i, c):
+            for u in range(n_q):
+                raw[n_kv + u] = jnp.dot(xn[...], slab[pl.ds(mult((n_kv + u + i) * D, 256), D), :], preferred_element_type=F32).astype(BF)
+            return c
+
+        lax.fori_loop(0, tp // tp_size + 1, queries, 0)
         for slot in range(GU_SLOTS):
             start_gu(slot, slot)
         for n in range(n_first):
@@ -259,6 +271,14 @@
             return c
 
         lax.fori_loop(0, CK // CH, insert, 0)
+        inner = side >= 2
+
+        @pl.when(inner)
+        def _():
+            got(0)
+            kx[5].start()
+            kx[7].start()
+
         kn_out = pltpu.make_async_copy(kcs, kn_o, o_sem.at[0])
         vn_out = pltpu.make_async_copy(vcs, vn_o, o_sem.at[1])
         kn_out.start()
@@ -280,50 +300,51 @@
         p_dec = (e_dec / jnp.sum(e_dec, axis=-1, keepdims=True)).astype(BF)
         c_dec = jnp.dot(p_dec, vcs[...], preferred_element_type=F32).astype(BF)
         for h in range(heads_local):
-            dcs[:, pl.ds(h * HD, HD)] = c_dec[h * B:(h + 1) * B]
+            dcs[h // rep, :, pl.ds((h % rep) * HD, HD)] = c_dec[h * B:(h + 1) * B]
         dec_rows = pl.ds(mult(2 * RT + core * B, B), B)
         hops = (2, 1, 3, 0)
         srcs = (2, 3, 1)
-        dx = [remote(dcs, ctxr.at[tp, dec_rows, :], dx_s.at[k], dx_r.at[k], side, at(hops[k])) for k in range(3)]
+        dec_at = lambda t, rows_: ctxr.at[:, rows_, pl.ds(mult(t * hw, 128), hw)]
+        dx = [remote(dcs, dec_at(tp, dec_rows), dx_s.at[k], dx_r.at[k], side, at(hops[k])) for k in range(3)]
         for cp in dx:
             cp.start()
-        ctxr[tp, dec_rows, :] = dcs[...]
-        df_own = remote(dcs, ctxr.at[tp, dec_rows, :], df_s.at[3], df_r.at[3], partner, tp)
+        dec_at(tp, dec_rows)[...] = dcs[...]
+        df_own = remote(dcs, dec_at(tp, dec_rows), df_s.at[3], df_r.at[3], partner, tp)
         df_own.start()
 
-        got(0)
-        kx[5].start()
-        kx[7].start()
-
+        win = []
+        for k in range(4):
+            r0 = mult(at(hops[k]) * RT, RT)
+            lead = side * R + r0 - max_req
+            lead = lead * ((lead + 2 * nblk * R) // (2 * nblk * R))
+            win.append((r0, mult(lead, RT)))
+            q_row = side * R + r0 + lax.broadcasted_iota(jnp.int32, (RT, 1), 0)
+            key_row = lead + lax.broadcasted_iota(jnp.int32, (1, WK), 1)
+            bias_s[k] = jnp.where((key_row >= seg_of(q_row)) & (key_row <= q_row), 0.0, -1e30)
         got(2)
-        got(5)
-
-        blks = [lax.rem(side + side_size - 2, side_size), lax.rem(side + side_size - 1, side_size), side]
+
+        @pl.when(inner)
+        def _():
+            got(5)
+
         pre_rows = pl.ds(mult(core * RT, RT), RT)
-        key_row = (side - 2) * R + lax.broadcasted_iota(jnp.int32, (1, 3 * R), 1)
         QR = rep * RT
-        q_off = lax.rem(lax.broadcasted_iota(jnp.int32, (QR, 1), 0), RT)
 
         def attend(j, k):
-            r0 = mult(at(hops[k]) * RT, RT)
-            q_row = side * R + r0 + q_off
-            q_seg = seg_of(q_row)
+            r0, lead = win[k]
             q = qs[pl.ds(j * rep, rep), pl.ds(r0, RT), :].reshape(QR, HD)
-            held = lambda i, b: kva[j, pl.ds(mult(b * R, R), R), pl.ds(i * HD, HD)]
-            s = jnp.concatenate([lax.dot_general(q, held(0, b), (((1,), (1,)), ((), ())), preferred_element_type=F32)
-                                 for b in blks], axis=-1) * scale
-            s = jnp.where((key_row >= q_seg) & (key_row <= q_row), s, -1e30)
+            held = lambda i: kva[j, pl.ds(lead, WK), pl.ds(i * HD, HD)]
+            s = lax.dot_general(q, held(0), (((1,), (1,)), ((), ())), preferred_element_type=F32)
+            s = s.reshape(rep, RT, WK) * scale + bias_s[k][None]
             e = jnp.exp(s - jnp.max(s, axis=-1, keepdims=True))
-            p = (e * (1.0 / jnp.sum(e, axis=-1, keepdims=True))).astype(BF)
-            o = jnp.zeros((QR, HD), F32)
-            for i, b in enumerate(blks):
-                o = o + jnp.dot(p[:, i * R:(i + 1) * R], held(1, b), preferred_element_type=F32)
+            p = (e * (1.0 / jnp.sum(e, axis=-1, keepdims=True))).astype(BF).reshape(QR, WK)
+            o = jnp.dot(p, held(1), preferred_element_type=F32)
             o = o.astype(BF)
             for h in range(rep):
                 cst[j, k, :, pl.ds(h * HD, HD)] = o[h * RT:(h + 1) * RT]
 
         def ctx_at(t, rows_, j):
-            return ctxr.at[t, rows_, pl.ds(j * hw, hw)]
+            return ctxr.at[j, rows_, pl.ds(mult(t * hw, 128), hw)]
 
         cx = [[remote(cst.at[j, k], ctx_at(tp, pre_rows, j), cx_s.at[j, k], cx_r.at[j, k], side, at(hops[k]))
                for k in range(3)] for j in range(2)]
@@ -343,25 +364,27 @@
                 if k < 3:
                     cx[j][k].start()
                 else:
-                    ctxr[tp, pre_rows, pl.ds(j * hw, hw)] = cst[j, 3]
+                    ctx_at(tp, pre_rows, j)[...] = cst[j, 3]
                     cf[j][3].start()
                 if j == 0 and k == 2:
-                    got(1)
-                    kx[6].start()
-                if j == 1 and k > 0:
-                    pass_ctx(0, k - 1)
+                    @pl.when(inner)
+                    def _():
+                        got(1)
+                        kx[6].start()
             if j == 0:
-                for k in range(3):
-                    ref = ctxr.at[at(srcs[k]), dec_rows, :]
-                    pltpu.make_async_copy(ref, ref, dx_r.at[k]).wait()
-                    df.append(remote(ref, ref, df_s.at[k], df_r.at[k], partner, tp))
-                    df[k].start()
                 got(3)
-                got(6)
-                got(4)
-                kx[8].start()
-                kx[9].start()
-
+
+                @pl.when(inner)
+                def _():
+                    got(6)
+
+        for k in range(3):
+            pass_ctx(0, k)
+        for k in range(3):
+            ref = dec_at(at(srcs[k]), dec_rows)
+            pltpu.make_async_copy(ref, ref, dx_r.at[k]).wait()
+            df.append(remote(ref, ref, df_s.at[k], df_r.at[k], partner, tp))
+            df[k].start()
         for k in range(3):
             pass_ctx(1, k)
         p_pre = pl.ds(mult(oc * RT, RT), RT)
@@ -371,7 +394,7 @@
             for j in range(2):
                 ref = ctx_at(t, p_pre, j)
                 pltpu.make_async_copy(ref, ref, cf_r.at[j, k]).wait()
-            ref = ctxr.at[t, p_dec_rows, :]
+            ref = dec_at(t, p_dec_rows)
             pltpu.make_async_copy(ref, ref, df_r.at[k]).wait()
         for cp in xres_l:
             cp.wait()
@@ -386,22 +409,37 @@
             ref = hf.at[:, pl.ds(mult(core * DH + u * CW, CW), CW)]
             return remote(ref, ref, h_s.at[u], h_r.at[u], partner, tp)
 
-        def out_proj(u, c):
-            base = wo_base + u * Q
-            slab_wait(mult(base, 256), Q, w_sem.at[n_kv + n_q + u])
-            acc = jnp.zeros((M2, CW), F32)
-            for t in range(tp_size):
-                acc = acc + jnp.dot(ctxr[t], slab[pl.ds(mult(base + t * qw, 256), qw), :], preferred_element_type=F32)
-            res = xres[:, pl.ds(mult(u * CW, CW), CW)].astype(F32)
-            hf[:, pl.ds(mult(core * DH + u * CW, CW), CW)] = (res + acc.astype(BF).astype(F32)).astype(BF)
-            h_copy(u).start()
-            return c
-
-        lax.fori_loop(0, n_o, out_proj, 0)
-        for i in (7, 9):
-            got(i)
-        kx[10].start()
-        kx[11].start()
+        OU = 2
+
+        def out_proj(i, c):
+            for k in range(OU):
+                u = i * OU + k
+                slab_wait(mult(wo_base + u * Q, 256), Q, w_sem.at[n_kv + n_q + u])
+            for k in range(OU):
+                u = i * OU + k
+                acc = jnp.zeros((M2, CW), F32)
+                for j in range(2):
+                    acc = acc + jnp.dot(ctxr[j], slab[pl.ds(mult(wo_base + u * Q + j * (Q // 2), 256), Q // 2), :],
+                                        preferred_element_type=F32)
+                res = xres[:, pl.ds(mult(u * CW, CW), CW)].astype(F32)
+                hf[:, pl.ds(mult(core * DH + u * CW, CW), CW)] = (res + acc.astype(BF).astype(F32)).astype(BF)
+            for k in range(OU):
+                h_copy(i * OU + k).start()
+            return c
+
+        lax.fori_loop(0, n_o // OU, out_proj, 0)
+        @pl.when(side < 2)
+        def _():
+            for i in (0, 1):
+                got(i)
+            for i in (5, 6, 7):
+                kx[i].start()
+            for i in (5, 6):
+                got(i)
+
+        got(4)
+        kx[8].start()
+        kx[9].start()
         for u in range(n_o):
             ref = hf.at[:, pl.ds(mult(oc * DH + u * CW, CW), CW)]
             pltpu.make_async_copy(ref, ref, h_r.at[u]).wait()
@@ -411,7 +449,7 @@
             hn[r, :] = norm(hf[r, :])
             return c
 
-        lax.fori_loop(0, M2 // 32, norm_h, 0)
+        lax.fori_loop(0, M2 // 32, norm_h, 0, unroll=True)
 
         def act_at(c_of, j):
             g = c_of * n_g + j
@@ -428,28 +466,40 @@
             slot = (top - 1) // (2 * D)
             return slot + ((n_g - 1 - slot) // GU_SLOTS) * GU_SLOTS
 
-        def gate_up(j, c):
-            slot = lax.rem(j, GU_SLOTS)
-            base = mult(gu_base + slot * (2 * D), 256)
-            slab_wait(base, 2 * D, g_sem.at[slot])
-            g = jnp.dot(hn[...], slab[pl.ds(base, D), :], preferred_element_type=F32)
-            u = jnp.dot(hn[...], slab[pl.ds(mult(base + D, 256), D), :], preferred_element_type=F32)
-            g = g.astype(BF).astype(F32)
-            u = u.astype(BF).astype(F32)
-            act_at(core, j)[...] = (g * jax.nn.sigmoid(g) * u).astype(BF)
-            a_copy(j).start()
-
+        def gu_base_of(j):
+            return mult(gu_base + lax.rem(j, GU_SLOTS) * (2 * D), 256)
+
+        def gu_next(j):
             @pl.when(j + GU_SLOTS < n_g)
             def _():
-                start_gu(j + GU_SLOTS, slot)
+                start_gu(j + GU_SLOTS, lax.rem(j, GU_SLOTS))
 
             for n in range(n_first, n_d):
                 @pl.when(j == last_slot(n))
                 def _(n=n):
                     d_copy(n).start()
-            return c
-
-        lax.fori_loop(0, n_g, gate_up, 0)
+
+        GU = 2
+
+        def gate_up(i, c):
+            for k in range(GU):
+                j = i * GU + k
+                slab_wait(gu_base_of(j), 2 * D, g_sem.at[lax.rem(j, GU_SLOTS)])
+            for k in range(GU):
+                j = i * GU + k
+                base = gu_base_of(j)
+                g = jnp.dot(hn[...], slab[pl.ds(base, D), :], preferred_element_type=F32)
+                u = jnp.dot(hn[...], slab[pl.ds(mult(base + D, 256), D), :], preferred_element_type=F32)
+                g = g.astype(BF).astype(F32)
+                u = u.astype(BF).astype(F32)
+                act_at(core, j)[...] = (g * jax.nn.sigmoid(g) * u).astype(BF)
+            for k in range(GU):
+                a_copy(i * GU + k).start()
+            for k in range(GU):
+                gu_next(i * GU + k)
+            return c
+
+        lax.fori_loop(0, n_g // GU, gate_up, 0)
 
         def a_got(j, c):
             ref = act_at(oc, j)
@@ -457,6 +507,11 @@
             return c
 
         lax.fori_loop(0, n_g, a_got, 0)
+
+        for i in (7, 9):
+            got(i)
+        kx[10].start()
+        kx[11].start()
 
         up, down = at(1), at(tp_size - 1)
         own_out = pl.ds(mult(core * RT, RT), RT)
@@ -493,8 +548,8 @@
 
         lax.fori_loop(0, n_d, down_proj, 0)
 
-        def piece(t, c_from, n):
-            return hid.at[rows_of(t), pl.ds(mult(c_from * DH + n * CW, CW), CW)]
+        def piece(t, c_from, n, of=hid):
+            return of.at[rows_of(t), pl.ds(mult(c_from * DH + n * CW, CW), CW)]
 
         def arrived(ref, sem):
             pltpu.make_async_copy(ref, ref, sem).wait()
@@ -507,11 +562,11 @@
                 if n % 2 == 0:
                     ref = piece(down, c_from, n)
                     arrived(ref, f_r.at[kind[(0, same)], n])
-                    cp = remote(ref, ref, r_s.at[same, n], r_r.at[same, n], side, up)
+                    cp = remote(ref, piece(down, c_from, n, hid_o), r_s.at[same, n], r_r.at[same, n], side, up)
                 else:
                     ref = piece(up, c_from, n)
                     arrived(ref, f_r.at[kind[(1, same)], n])
-                    cp = remote(ref, ref, r_s.at[same, n], r_r.at[same, n], side, down)
+                    cp = remote(ref, piece(up, c_from, n, hid_o), r_s.at[same, n], r_r.at[same, n], side, down)
                 cp.start()
                 relays.append(cp)
 
@@ -565,8 +620,7 @@
         flush(down, 2)
         for n in range(n_d):
             for same in (1, 0):
-                arrived(piece(at(2), core if same else oc, n), r_r.at[same, n])
-        flush(at(2), 3)
+                arrived(piece(at(2), core if same else oc, n, hid_o), r_r.at[same, n])
 
         for cp in kx + dx + df + [df_own] + cx[0] + cx[1] + cf[0] + cf[1] + relays:
             cp.wait_send()
@@ -594,17 +648,18 @@
 
     dma = lambda *s: pltpu.SemaphoreType.DMA(s)
     scratch = [
+        pltpu.SMEM((side_size,), jnp.int32), pltpu.SMEM((side_size,), jnp.int32), pltpu.SMEM((B,), jnp.int32), pltpu.VMEM((8, HD), F32),
         pltpu.VMEM((slab_rows, CW), BF),
         pltpu.VMEM((max(R + M1, -(-F // D) * M2), D), BF), pltpu.VMEM((B, D), BF),
         pltpu.VMEM((n_kv + n_q, M1, CW), BF), pltpu.VMEM((heads_local, M1, HD), BF),
         pltpu.VMEM((2, nblk * R, 2 * HD), BF), pltpu.VMEM((2 * B, 3 * HD), BF),
         pltpu.VMEM((CK, HD), BF), pltpu.VMEM((CK, HD), BF),
-        pltpu.VMEM((M1, HD), F32), pltpu.VMEM((M1, HD), F32),
-        pltpu.VMEM((B, qw), BF), pltpu.VMEM((2, 4, RT, hw), BF), pltpu.VMEM((tp_size, M2, qw), BF),
+        pltpu.VMEM((M1, HD), F32), pltpu.VMEM((M1, HD), F32), pltpu.VMEM((4, RT, max_req + RT), F32),
+        pltpu.VMEM((2, B, hw), BF), pltpu.VMEM((2, 4, RT, hw), BF), pltpu.VMEM((2, M2, Q // 2), BF),
         pltpu.VMEM((M2, DH), BF), pltpu.VMEM((M2, D), BF), pltpu.VMEM((M2, D), BF),
         pltpu.VMEM((n_d, M2, CW), BF), pltpu.VMEM((R, D), BF), pltpu.VMEM((B, D), BF),
         pltpu.VMEM((PR, HD), BF), pltpu.VMEM((PR, HD), BF),
-        dma(6), dma(n_kv + n_q + n_o), dma(GU_SLOTS), dma(n_d),
+        dma(14), dma(n_kv + n_q + n_o), dma(GU_SLOTS), dma(n_d),
         dma(2), dma(2), dma(12), dma(12), dma(2, 3), dma(2, 3), dma(2, 4), dma(2, 4),
         dma(3), dma(3), dma(4), dma(4), dma(n_o), dma(n_o), dma(n_g), dma(n_g),
         dma(6, n_d), dma(6, n_d), dma(2, n_d), dma(2, n_d), dma(9),
@@ -669,14 +724,13 @@
         table[1] = np.concatenate([-np.ones(half), np.ones(half)])
         fq = jnp.asarray(table)
         any_spec = pl.BlockSpec(memory_space=pl.ANY)
-        smem = pl.BlockSpec(memory_space=pltpu.SMEM)
         CK = B * T * slots
         hid, dec, kp, vp, kn, vn = pl.pallas_call(
             kernel,
             name='prefill_decode',
             out_shape=[jax.ShapeDtypeStruct(s, BF) for s in
                        ((R, D), (B, D), (max_req * 2, HD), (max_req * 2, HD), (CK, HD), (CK, HD))],
-            in_specs=[any_spec] * 9 + [smem] * 3 + [pl.BlockSpec(memory_space=pltpu.VMEM)],
+            in_specs=[any_spec] * 13,
             out_specs=[any_spec] * 6,
             scratch_shapes=scratch,
             compiler_params=pltpu.CompilerParams(collective_id=0, has_side_effects=True, vmem_limit_bytes=67043328),

time: 67.6 us -> 62.2 us (0.920); the launches traced: 67.5 us -> 61.3 us
  Pallas kernels: 66.8 us -> 60.7 us
    pallas_call x1, Pallas kernels: 64 us -> 57.9 us  [local_step(): pl.pallas_call(kernel, name='prefill_decode', out_shape=[jax.ShapeDtypeSt...]
where the time goes in v3:
time: 62.2 us; the launch traced here: 61.3 us
  Pallas kernels  60.7 us (98%)
  between operations  0.64 us (1%)
    pallas_call x1, Pallas kernels, local_step(): pl.pallas_call(kernel, name='prefill_decode', out_shape=[jax.ShapeDtypeSt...  57.9 us
    pallas_call x1, Pallas kernels, write_out(): pl.pallas_call(kernel, name='write_out', out_shape=[jax.ShapeDtypeStruct(...  2.82 us

profile of v3, /device:TPU:97, one launch (start us, length us, event | category | flops | bytes accessed | tf_op | source)
XLA Modules:
  0.0 61.3 jit_solution(3769985718717641170)
XLA Ops:
  0.6 57.9 %prefill_decode.1 = (bf16[256,3072]{1,0:T(8,128)(2,1)}, bf16[16,3072]{1,0:T(8,128)(2,1)}, bf16[896,128]{1,0:T(8,128)(2,1)}, bf16[896,128]{1,0:T(8,128)(2,1)}, bf...) custom-call(bf16[256,3072]{1,0:T(8,128)(2,1)} %x_h.1, bf16[16,3072]{1,0:T(8,128)(2,1)} %bitcast.21, ...), custom_call_target="tpu_custom_call" | custom-call | tf_op jit(solution)/shard_map/prefill_decode/pallas_call | solution.py:728
  58.5 2.8 %write_out.1 = (bf16[256,3072]{1,0:T(8,128)(2,1)}, bf16[16,3072]{1,0:T(8,128)(2,1)}, bf16[896,128]{1,0:T(8,128)(2,1)}, bf16[896,128]{1,0:T(8,128)(2,1)}, bf16[20...) custom-call(bf16[256,3072]{1,0:T(8,128)(2,1)} %get-tuple-element.18.refs_0_, bf16[16,3072]{1,0:T(8,128)(2,1)} %get-tuple-element.19.refs_1_, ...), custom_call_target="tpu_custom_call" | custom-call | tf_op jit(solution)/shard_map/write_out/pallas_call | solution.py:693

commit v4 on v3

--- a/solution.py
+++ b/solution.py
@@ -11,7 +11,7 @@
 BF = jnp.bfloat16
 F32 = jnp.float32
 CW = 256
-GU_SLOTS = 9
+GU_SLOTS = 10
 MESH = pl.DeviceIdType.MESH
 
 
@@ -39,13 +39,14 @@
     scale = HD ** -0.5
     WK = max_req + RT
     n_first = wo_base // F
-    AB = D // CW
+    AW = max(w for w in range(CW, D + 1, CW) if FH % w == 0)
+    AB, AN = AW // CW, FH // AW
     nblk = side_size
 
     def kernel(x_h, y_h, wqkv_h, wo_h, wg_h, wu_h, wd_h, kc_h, vc_h, rl_h, dst_h, cl_h, fq_h,
                hid_o, dec_o, kp_o, vp_o, kn_o, vn_o,
                rl, dst, cl, fq, slab, ub, ys, raw, qs, kva, knv, kcs, vcs, cos_s, sin_s, bias_s,
-               dcs, cst, ctxr, xres, hf, hn, outst, hid, decb, kps, vps,
+               dcs, cst, ctxr, xres, hf, outst, hid, decb,
                in_sem, w_sem, g_sem, d_sem, xr_s, xr_r, kx_s, kx_r, cx_s, cx_r, cf_s, cf_r,
                dx_s, dx_r, df_s, df_r, h_s, h_r, a_s, a_r, f_s, f_r, r_s, r_r, o_sem):
         xs, xn = ub.at[pl.ds(0, R), :], ub.at[pl.ds(R, M1), :]
@@ -114,8 +115,6 @@
         y_in = pltpu.make_async_copy(y_h, ys, in_sem.at[1])
         for cp in small + x_in + [y_in]:
             cp.start()
-        for u in range(n_kv + n_q):
-            start_qkv(u)
 
         peers = [(partner, tp), (left, tp), (right, tp), (side, at(1)), (side, at(tp_size - 1)), (side, at(2)),
                  (partner, at(1)), (partner, at(tp_size - 1))]
@@ -125,16 +124,12 @@
 
         kc_in = pltpu.make_async_copy(kc_h, kcs, in_sem.at[2])
         vc_in = pltpu.make_async_copy(vc_h, vcs, in_sem.at[3])
-        kc_in.start()
-        vc_in.start()
         row_t = mult(tp * RT, RT)
         my_cols = mult(core * DH, 128)
         xres_l = [pltpu.make_async_copy(x_h.at[pl.ds(row_t, RT), pl.ds(my_cols, DH)],
                                         xres.at[pl.ds(mult(core * RT, RT), RT), :], in_sem.at[4]),
                   pltpu.make_async_copy(y_h.at[:, pl.ds(my_cols, DH)],
                                         xres.at[pl.ds(mult(2 * RT + core * B, B), B), :], in_sem.at[5])]
-        for cp in xres_l:
-            cp.start()
 
         def seg_of(rows):
             seg = jnp.zeros_like(rows)
@@ -162,6 +157,7 @@
 
         for i in range(XC):
             x_in[i].wait()
+            start_qkv(i)
 
             def norm_x(k, c, i=i):
                 r = pl.ds(mult(i * (R // XC) + k * 32, 32), 32)
@@ -169,6 +165,8 @@
                 return c
 
             lax.fori_loop(0, R // XC // 32, norm_x, 0, unroll=True)
+        for u in range(XC, n_kv + n_q):
+            start_qkv(u)
         y_in.wait()
         xn[pl.ds(R, B), :] = norm(ys[...])
 
@@ -184,14 +182,12 @@
 
         def project(u):
             w = slab[pl.ds(mult(u * D, 256), D), :]
-            raw[u] = jnp.dot(xn[...], w, preferred_element_type=F32).astype(BF)
+            raw[pl.ds(mult(u * M1, 16), M1), :] = jnp.dot(xn[...], w, preferred_element_type=F32).astype(BF)
 
         def rope(v):
             w = v.astype(F32)
             return (w * cos_s[...] + pltpu.roll(w, HD // 2, 1) * sin_s[...]).astype(BF)
 
-        for u in range(n_o):
-            start_wo(u)
 
         def blk(b, i0, n):
             return kva.at[pl.ds(i0, n), pl.ds(mult(b * R, R), R), :]
@@ -216,8 +212,8 @@
         def keys_values(j, c):
             slab_wait(mult(j * D, 256), D, w_sem.at[j])
             project(j)
-            k_j = rope(raw[j, :, pl.ds(0, HD)])
-            v_j = raw[j, :, pl.ds(HD, HD)]
+            k_j = rope(raw[pl.ds(mult(j * M1, 16), M1), pl.ds(0, HD)])
+            v_j = raw[pl.ds(mult(j * M1, 16), M1), pl.ds(HD, HD)]
             kva[j, own_rows, pl.ds(0, HD)] = k_j[:R]
             kva[j, own_rows, pl.ds(HD, HD)] = v_j[:R]
             ref = blk(side, j, 1)
@@ -233,12 +229,16 @@
             cp.start()
         knv[:, pl.ds(2 * HD, HD)] = jnp.ones((2 * B, HD), BF)
 
+        for cp in [kc_in, vc_in] + xres_l:
+            cp.start()
+        for u in range(n_o):
+            start_wo(u)
         for u in range(n_kv, n_kv + n_q):
             slab_wait(u * D, D, w_sem.at[u])
 
         def queries(i, c):
             for u in range(n_q):
-                raw[n_kv + u] = jnp.dot(xn[...], slab[pl.ds(mult((n_kv + u + i) * D, 256), D), :], preferred_element_type=F32).astype(BF)
+                raw[pl.ds((n_kv + u) * M1, M1), :] = jnp.dot(xn[...], slab[pl.ds(mult((n_kv + u + i) * D, 256), D), :], preferred_element_type=F32).astype(BF)
             return c
 
         lax.fori_loop(0, tp // tp_size + 1, queries, 0)
@@ -248,7 +248,7 @@
             d_copy(n).start()
         for h in range(heads_local):
             u, off = divmod(h * HD, CW)
-            qs[h] = rope(raw[2 + u, :, pl.ds(off, HD)])
+            qs[h] = rope(raw[pl.ds((n_kv + u) * M1, M1), pl.ds(off, HD)])
 
         kc_in.wait()
         vc_in.wait()
@@ -320,7 +320,9 @@
             win.append((r0, mult(lead, RT)))
             q_row = side * R + r0 + lax.broadcasted_iota(jnp.int32, (RT, 1), 0)
             key_row = lead + lax.broadcasted_iota(jnp.int32, (1, WK), 1)
-            bias_s[k] = jnp.where((key_row >= seg_of(q_row)) & (key_row <= q_row), 0.0, -1e30)
+            bias = jnp.where((key_row >= seg_of(q_row)) & (key_row <= q_row), 0.0, -1e30)
+            for i in range(WK // CW):
+                bias_s[i, pl.ds(k * RT, RT), :] = bias[:, i * CW:(i + 1) * CW]
         got(2)
 
         @pl.when(inner)
@@ -335,7 +337,7 @@
             q = qs[pl.ds(j * rep, rep), pl.ds(r0, RT), :].reshape(QR, HD)
             held = lambda i: kva[j, pl.ds(lead, WK), pl.ds(i * HD, HD)]
             s = lax.dot_general(q, held(0), (((1,), (1,)), ((), ())), preferred_element_type=F32)
-            s = s.reshape(rep, RT, WK) * scale + bias_s[k][None]
+            s = s.reshape(rep, RT, WK) * scale + jnp.concatenate([bias_s[i, pl.ds(k * RT, RT), :] for i in range(WK // CW)], axis=-1)[None]
             e = jnp.exp(s - jnp.max(s, axis=-1, keepdims=True))
             p = (e * (1.0 / jnp.sum(e, axis=-1, keepdims=True))).astype(BF).reshape(QR, WK)
             o = jnp.dot(p, held(1), preferred_element_type=F32)
@@ -360,7 +362,9 @@
         df = []
         for j in range(2):
             for k in range(4):
-                attend(j, k)
+                if k % 2 == 0:
+                    attend(j, k)
+                    attend(j, k + 1)
                 if k < 3:
                     cx[j][k].start()
                 else:
@@ -425,6 +429,11 @@
                 hf[:, pl.ds(mult(core * DH + u * CW, CW), CW)] = (res + acc.astype(BF).astype(F32)).astype(BF)
             for k in range(OU):
                 h_copy(i * OU + k).start()
+            for n in range(n_first, n_d):
+                if (n + 1) * F <= gu_base:
+                    @pl.when(i == (min((n + 1) * F - wo_base, n_o * Q) - 1) // (OU * Q))
+                    def _(n=n):
+                        d_copy(n).start()
             return c
 
         lax.fori_loop(0, n_o // OU, out_proj, 0)
@@ -444,9 +453,14 @@
             ref = hf.at[:, pl.ds(mult(oc * DH + u * CW, CW), CW)]
             pltpu.make_async_copy(ref, ref, h_r.at[u]).wait()
 
+        for cp in df + [df_own] + cf[0] + cf[1]:
+            cp.wait_send()
+
         def norm_h(i, c):
             r = pl.ds(mult(i * 32, 32), 32)
-            hn[r, :] = norm(hf[r, :])
+            v = norm(hf[r, :])
+            for j in range(2):
+                ctxr[j, r, :] = v[:, j * DH:(j + 1) * DH]
             return c
 
         lax.fori_loop(0, M2 // 32, norm_h, 0, unroll=True)
@@ -461,8 +475,6 @@
 
         def last_slot(n):
             top = (n + 1) * F - gu_base
-            if top <= 0:
-                return 2 * (n - n_first) + 2
             slot = (top - 1) // (2 * D)
             return slot + ((n_g - 1 - slot) // GU_SLOTS) * GU_SLOTS
 
@@ -474,7 +486,7 @@
             def _():
                 start_gu(j + GU_SLOTS, lax.rem(j, GU_SLOTS))
 
-            for n in range(n_first, n_d):
+            for n in range(gu_base // F, n_d):
                 @pl.when(j == last_slot(n))
                 def _(n=n):
                     d_copy(n).start()
@@ -488,8 +500,9 @@
             for k in range(GU):
                 j = i * GU + k
                 base = gu_base_of(j)
-                g = jnp.dot(hn[...], slab[pl.ds(base, D), :], preferred_element_type=F32)
-                u = jnp.dot(hn[...], slab[pl.ds(mult(base + D, 256), D), :], preferred_element_type=F32)
+                half = lambda i: slab[pl.ds(mult(base + i * DH, 256), DH), :]
+                g = jnp.dot(ctxr[0], half(0), preferred_element_type=F32) + jnp.dot(ctxr[1], half(1), preferred_element_type=F32)
+                u = jnp.dot(ctxr[0], half(2), preferred_element_type=F32) + jnp.dot(ctxr[1], half(3), preferred_element_type=F32)
                 g = g.astype(BF).astype(F32)
                 u = u.astype(BF).astype(F32)
                 act_at(core, j)[...] = (g * jax.nn.sigmoid(g) * u).astype(BF)
@@ -505,8 +518,6 @@
             ref = act_at(oc, j)
             pltpu.make_async_copy(ref, ref, a_r.at[j]).wait()
             return c
-
-        lax.fori_loop(0, n_g, a_got, 0)
 
         for i in (7, 9):
             got(i)
@@ -531,22 +542,45 @@
                     remote(his, there, f_s.at[4, n], f_r.at[4, n], partner, tp),
                     remote(outst.at[n, his_dec, :], decb.at[:, cols], f_s.at[5, n], f_r.at[5, n], partner, tp)]
 
-        def down_proj(n, c):
-            d_copy(n).wait()
-            acc = jnp.zeros((M2, CW), F32)
-            for i in range(-(-F // D)):
-                w = min(D, F - i * D)
-                acc = acc + jnp.dot(ub[pl.ds(i * M2, M2), pl.ds(0, w)], slab[pl.ds(mult(n * F + i * D, 256), w), :],
-                                    preferred_element_type=F32)
+        def down_part(n, c_of):
+            acc = None
+            for i in range(AN):
+                g = c_of * AN + i
+                part = jnp.dot(ub[pl.ds(mult(g * M2, 16), M2), pl.ds(0, AW)],
+                               slab[pl.ds(mult(n * F + g * AW, 256), AW), :], preferred_element_type=F32)
+                acc = part if acc is None else acc + part
+            return acc
+
+        def down_end(n, acc):
             cols = pl.ds(mult(core * DH + n * CW, CW), CW)
             outst[n] = (hf[:, cols].astype(F32) + acc.astype(BF).astype(F32)).astype(BF)
             for cp in f_copies(n):
                 cp.start()
             hid[rows_of(tp), cols] = outst[n, own_out, :]
             decb[:, cols] = outst[n, own_dec, :]
-            return c
-
-        lax.fori_loop(0, n_d, down_proj, 0)
+
+        EARLY = 2
+
+        def down_first(n, c):
+            d_copy(n).wait()
+            bias_s[n, pl.ds(0, M2), :] = down_part(n, core)
+            return c
+
+        lax.fori_loop(0, EARLY, down_first, 0)
+        lax.fori_loop(0, n_g, a_got, 0)
+
+        def down_second(n, c):
+            down_end(n, bias_s[n, pl.ds(0, M2), :] + down_part(n, oc))
+            return c
+
+        lax.fori_loop(0, EARLY, down_second, 0)
+
+        def down_proj(n, c):
+            d_copy(n).wait()
+            down_end(n, down_part(n, core) + down_part(n, oc))
+            return c
+
+        lax.fori_loop(EARLY, n_d, down_proj, 0)
 
         def piece(t, c_from, n, of=hid):
             return of.at[rows_of(t), pl.ds(mult(c_from * DH + n * CW, CW), CW)]
@@ -587,12 +621,11 @@
             code = jnp.where(o_row // 2 < length, o_row // 2 + start + lax.rem(o_row, 2) * (nblk * R), -1)
             pick = jnp.where(code == col, 1.0, 0.0).astype(BF)
             out = jnp.dot(pick, kva[...].reshape(2 * nblk * R, 2 * HD), preferred_element_type=F32).astype(BF)
-            kps[r, :] = out[:, :HD]
-            vps[r, :] = out[:, HD:]
+            raw[r, :] = out
             return c
 
         lax.fori_loop(0, PR // IR, install, 0)
-        outs = [pltpu.make_async_copy(kps, kp_o, o_sem.at[2]), pltpu.make_async_copy(vps, vp_o, o_sem.at[3])]
+        outs = [pltpu.make_async_copy(raw.at[pl.ds(0, PR), pl.ds(i * HD, HD)], o, o_sem.at[2 + i]) for i, o in enumerate((kp_o, vp_o))]
         for cp in outs:
             cp.start()
 
@@ -622,7 +655,7 @@
             for same in (1, 0):
                 arrived(piece(at(2), core if same else oc, n, hid_o), r_r.at[same, n])
 
-        for cp in kx + dx + df + [df_own] + cx[0] + cx[1] + cf[0] + cf[1] + relays:
+        for cp in kx + dx + cx[0] + cx[1] + relays:
             cp.wait_send()
 
         def h_done(u, c):
@@ -650,15 +683,14 @@
     scratch = [
         pltpu.SMEM((side_size,), jnp.int32), pltpu.SMEM((side_size,), jnp.int32), pltpu.SMEM((B,), jnp.int32), pltpu.VMEM((8, HD), F32),
         pltpu.VMEM((slab_rows, CW), BF),
-        pltpu.VMEM((max(R + M1, -(-F // D) * M2), D), BF), pltpu.VMEM((B, D), BF),
-        pltpu.VMEM((n_kv + n_q, M1, CW), BF), pltpu.VMEM((heads_local, M1, HD), BF),
+        pltpu.VMEM((max(R + M1, 2 * AN * M2), D), BF), pltpu.VMEM((B, D), BF),
+        pltpu.VMEM((max((n_kv + n_q) * M1, PR), CW), BF), pltpu.VMEM((heads_local, M1, HD), BF),
         pltpu.VMEM((2, nblk * R, 2 * HD), BF), pltpu.VMEM((2 * B, 3 * HD), BF),
         pltpu.VMEM((CK, HD), BF), pltpu.VMEM((CK, HD), BF),
-        pltpu.VMEM((M1, HD), F32), pltpu.VMEM((M1, HD), F32), pltpu.VMEM((4, RT, max_req + RT), F32),
+        pltpu.VMEM((M1, HD), F32), pltpu.VMEM((M1, HD), F32), pltpu.VMEM((WK // CW, max(4 * RT, M2), CW), F32),
         pltpu.VMEM((2, B, hw), BF), pltpu.VMEM((2, 4, RT, hw), BF), pltpu.VMEM((2, M2, Q // 2), BF),
-        pltpu.VMEM((M2, DH), BF), pltpu.VMEM((M2, D), BF), pltpu.VMEM((M2, D), BF),
+        pltpu.VMEM((M2, DH), BF), pltpu.VMEM((M2, D), BF),
         pltpu.VMEM((n_d, M2, CW), BF), pltpu.VMEM((R, D), BF), pltpu.VMEM((B, D), BF),
-        pltpu.VMEM((PR, HD), BF), pltpu.VMEM((PR, HD), BF),
         dma(14), dma(n_kv + n_q + n_o), dma(GU_SLOTS), dma(n_d),
         dma(2), dma(2), dma(12), dma(12), dma(2, 3), dma(2, 3), dma(2, 4), dma(2, 4),
         dma(3), dma(3), dma(4), dma(4), dma(n_o), dma(n_o), dma(n_g), dma(n_g),

time: 62.2 us -> 59.4 us (0.955); the launches traced: 61.3 us -> 59.2 us
  Pallas kernels: 60.7 us -> 58.4 us
    pallas_call x1, Pallas kernels: 57.9 us -> 55.6 us  [local_step(): pl.pallas_call(kernel, name='prefill_decode', out_shape=[jax.ShapeDtypeSt...]
where the time goes in v4:
time: 59.4 us; the launch traced here: 59.2 us
  Pallas kernels  58.4 us (98%)
  between operations  0.81 us (1%)
    pallas_call x1, Pallas kernels, local_step(): pl.pallas_call(kernel, name='prefill_decode', out_shape=[jax.ShapeDtypeSt...  55.6 us
    pallas_call x1, Pallas kernels, write_out(): pl.pallas_call(kernel, name='write_out', out_shape=[jax.ShapeDtypeStruct(...  2.82 us

profile of v4, /device:TPU:97, one launch (start us, length us, event | category | flops | bytes accessed | tf_op | source)
XLA Modules:
  0.0 59.2 jit_solution(15500288130068846850)
XLA Ops:
  0.6 55.6 %prefill_decode.1 = (bf16[256,3072]{1,0:T(8,128)(2,1)}, bf16[16,3072]{1,0:T(8,128)(2,1)}, bf16[896,128]{1,0:T(8,128)(2,1)}, bf16[896,128]{1,0:T(8,128)(2,1)}, bf...) custom-call(bf16[256,3072]{1,0:T(8,128)(2,1)} %x_h.1, bf16[16,3072]{1,0:T(8,128)(2,1)} %bitcast.21, ...), custom_call_target="tpu_custom_call" | custom-call | tf_op jit(solution)/shard_map/prefill_decode/pallas_call | solution.py:760
  56.3 2.8 %write_out.1 = (bf16[256,3072]{1,0:T(8,128)(2,1)}, bf16[16,3072]{1,0:T(8,128)(2,1)}, bf16[896,128]{1,0:T(8,128)(2,1)}, bf16[896,128]{1,0:T(8,128)(2,1)}, bf16[20...) custom-call(bf16[256,3072]{1,0:T(8,128)(2,1)} %get-tuple-element.18.refs_0_, bf16[16,3072]{1,0:T(8,128)(2,1)} %get-tuple-element.19.refs_1_, ...), custom_call_target="tpu_custom_call" | custom-call | tf_op jit(solution)/shard_map/write_out/pallas_call | solution.py:725

commit v5 on v4

--- a/solution.py
+++ b/solution.py
@@ -115,6 +115,7 @@
         y_in = pltpu.make_async_copy(y_h, ys, in_sem.at[1])
         for cp in small + x_in + [y_in]:
             cp.start()
+        start_qkv(0)
 
         peers = [(partner, tp), (left, tp), (right, tp), (side, at(1)), (side, at(tp_size - 1)), (side, at(2)),
                  (partner, at(1)), (partner, at(tp_size - 1))]
@@ -157,7 +158,7 @@
 
         for i in range(XC):
             x_in[i].wait()
-            start_qkv(i)
+            start_qkv(i + 1)
 
             def norm_x(k, c, i=i):
                 r = pl.ds(mult(i * (R // XC) + k * 32, 32), 32)
@@ -165,7 +166,7 @@
                 return c
 
             lax.fori_loop(0, R // XC // 32, norm_x, 0, unroll=True)
-        for u in range(XC, n_kv + n_q):
+        for u in range(XC + 1, n_kv + n_q):
             start_qkv(u)
         y_in.wait()
         xn[pl.ds(R, B), :] = norm(ys[...])
@@ -443,8 +444,6 @@
                 got(i)
             for i in (5, 6, 7):
                 kx[i].start()
-            for i in (5, 6):
-                got(i)
 
         got(4)
         kx[8].start()
@@ -603,6 +602,11 @@
                     cp = remote(ref, piece(up, c_from, n, hid_o), r_s.at[same, n], r_r.at[same, n], side, down)
                 cp.start()
                 relays.append(cp)
+
+        @pl.when(side < 2)
+        def _():
+            for i in (5, 6):
+                got(i)
 
         for i in (8, 10, 11):
             got(i)

time: 59.4 us -> 59 us (level)
  no operation moved by 1% of the time
where the time goes in v5:
time: 59 us; the launch traced here: 58.9 us
  Pallas kernels  58.1 us (98%)
  between operations  0.81 us (1%)
    pallas_call x1, Pallas kernels, local_step(): pl.pallas_call(kernel, name='prefill_decode', out_shape=[jax.ShapeDtypeSt...  55.2 us
    pallas_call x1, Pallas kernels, write_out(): pl.pallas_call(kernel, name='write_out', out_shape=[jax.ShapeDtypeStruct(...  2.82 us

profile of v5, /device:TPU:97, one launch (start us, length us, event | category | flops | bytes accessed | tf_op | source)
XLA Modules:
  0.0 58.9 jit_solution(1001575696334320824)
XLA Ops:
  0.6 55.2 %prefill_decode.1 = (bf16[256,3072]{1,0:T(8,128)(2,1)}, bf16[16,3072]{1,0:T(8,128)(2,1)}, bf16[896,128]{1,0:T(8,128)(2,1)}, bf16[896,128]{1,0:T(8,128)(2,1)}, bf...) custom-call(bf16[256,3072]{1,0:T(8,128)(2,1)} %x_h.1, bf16[16,3072]{1,0:T(8,128)(2,1)} %bitcast.21, ...), custom_call_target="tpu_custom_call" | custom-call | tf_op jit(solution)/shard_map/prefill_decode/pallas_call | solution.py:764
  55.9 2.8 %write_out.1 = (bf16[256,3072]{1,0:T(8,128)(2,1)}, bf16[16,3072]{1,0:T(8,128)(2,1)}, bf16[896,128]{1,0:T(8,128)(2,1)}, bf16[896,128]{1,0:T(8,128)(2,1)}, bf16[20...) custom-call(bf16[256,3072]{1,0:T(8,128)(2,1)} %get-tuple-element.18.refs_0_, bf16[16,3072]{1,0:T(8,128)(2,1)} %get-tuple-element.19.refs_1_, ...), custom_call_target="tpu_custom_call" | custom-call | tf_op jit(solution)/shard_map/write_out/pallas_call | solution.py:729

commit v6 on v5

--- a/solution.py
+++ b/solution.py
@@ -371,7 +371,7 @@
                 else:
                     ctx_at(tp, pre_rows, j)[...] = cst[j, 3]
                     cf[j][3].start()
-                if j == 0 and k == 2:
+                if j == 0 and k == 1:
                     @pl.when(inner)
                     def _():
                         got(1)
@@ -383,14 +383,14 @@
                 def _():
                     got(6)
 
-        for k in range(3):
+        for k in (1, 0, 2):
             pass_ctx(0, k)
         for k in range(3):
             ref = dec_at(at(srcs[k]), dec_rows)
             pltpu.make_async_copy(ref, ref, dx_r.at[k]).wait()
             df.append(remote(ref, ref, df_s.at[k], df_r.at[k], partner, tp))
             df[k].start()
-        for k in range(3):
+        for k in (1, 0, 2):
             pass_ctx(1, k)
         p_pre = pl.ds(mult(oc * RT, RT), RT)
         p_dec_rows = pl.ds(mult(2 * RT + oc * B, B), B)

time: 59 us -> 59 us (level)
  no operation moved by 1% of the time
where the time goes in v6:
time: 59 us; the launch traced here: 58.9 us
  Pallas kernels  58.1 us (98%)
  between operations  0.81 us (1%)
    pallas_call x1, Pallas kernels, local_step(): pl.pallas_call(kernel, name='prefill_decode', out_shape=[jax.ShapeDtypeSt...  55.2 us
    pallas_call x1, Pallas kernels, write_out(): pl.pallas_call(kernel, name='write_out', out_shape=[jax.ShapeDtypeStruct(...  2.82 us

profile of v6, /device:TPU:97, one launch (start us, length us, event | category | flops | bytes accessed | tf_op | source)
XLA Modules:
  0.0 58.9 jit_solution(10140722657842536117)
XLA Ops:
  0.6 55.2 %prefill_decode.1 = (bf16[256,3072]{1,0:T(8,128)(2,1)}, bf16[16,3072]{1,0:T(8,128)(2,1)}, bf16[896,128]{1,0:T(8,128)(2,1)}, bf16[896,128]{1,0:T(8,128)(2,1)}, bf...) custom-call(bf16[256,3072]{1,0:T(8,128)(2,1)} %x_h.1, bf16[16,3072]{1,0:T(8,128)(2,1)} %bitcast.21, ...), custom_call_target="tpu_custom_call" | custom-call | tf_op jit(solution)/shard_map/prefill_decode/pallas_call | solution.py:764
  55.9 2.8 %write_out.1 = (bf16[256,3072]{1,0:T(8,128)(2,1)}, bf16[16,3072]{1,0:T(8,128)(2,1)}, bf16[896,128]{1,0:T(8,128)(2,1)}, bf16[896,128]{1,0:T(8,128)(2,1)}, bf16[20...) custom-call(bf16[256,3072]{1,0:T(8,128)(2,1)} %get-tuple-element.18.refs_0_, bf16[16,3072]{1,0:T(8,128)(2,1)} %get-tuple-element.19.refs_1_, ...), custom_call_target="tpu_custom_call" | custom-call | tf_op jit(solution)/shard_map/write_out/pallas_call | solution.py:729
